TPU v7x, 128 devices: a whole 4x4x4 slice. The times are simulated.
128 devices in a mesh: rep: 1, fsdp: 2 (over core), ep: 64 (over z, y, x).
Axes of the slice: x: 4, y: 4, z: 4, core: 2. Of those that a mesh axis runs over, the one named last changes fastest.
Arguments:
- tokens: bfloat16 [32768, 2048], P(('rep', 'ep', 'fsdp'))
- expert_idx: int32 [32768, 6], P(('rep', 'ep', 'fsdp'))
- gates: float32 [32768, 6], P(('rep', 'ep', 'fsdp'))
- w_gate: bfloat16 [64, 2048, 1408], P('ep', 'fsdp')
- w_up: bfloat16 [64, 2048, 1408], P('ep', 'fsdp')
- w_down: bfloat16 [64, 1408, 2048], P('ep', None, 'fsdp')
Outputs:
- output: bfloat16 [32768, 2048], P(('rep', 'ep', 'fsdp'))
All inputs are finite; a program needn't handle non-finite values.
Results may differ from a plain program's by a relative error of at most 0.00138.
Values are sent between devices in bfloat16 or wider.
A program may use at most 1 GiB of HBM per device.

v0:
```python
import jax
import jax.numpy as jnp
from jax import lax
from jax.sharding import PartitionSpec as P


def routing_matrix(expert_idx, num_experts, capacity):
    tok_count, top_k = expert_idx.shape
    flat_ids = expert_idx.reshape(tok_count * top_k)
    onehot = (flat_ids[:, None] == jnp.arange(num_experts)[None, :]).astype(jnp.int32)
    before = jnp.cumsum(onehot, axis=0) - onehot
    slot_ids = jnp.sum(before * onehot, axis=1)
    target = jnp.where(slot_ids < capacity, flat_ids * capacity + slot_ids, -1)
    select = target[:, None] == jnp.arange(num_experts * capacity)[None, :]
    return select.astype(jnp.bfloat16).reshape(tok_count, top_k, num_experts * capacity)


def solution(mesh):
    ep_size = mesh.shape['ep']
    row_spec = P(('rep', 'ep', 'fsdp'), None)

    def device_step(tokens, expert_idx, gates, w_gate, w_up, w_down):
        tok_count, top_k = expert_idx.shape
        n_local = w_gate.shape[0]
        num_experts = n_local * ep_size
        model_dim = tokens.shape[1]
        capacity = (2 * tok_count * top_k + num_experts - 1) // num_experts
        select = routing_matrix(expert_idx, num_experts, capacity)
        send_buf = jnp.einsum('tkf,td->fd', select, tokens, preferred_element_type=jnp.float32).astype(jnp.bfloat16)
        send_buf = send_buf.reshape(ep_size, n_local, capacity, model_dim)
        recv_buf = lax.all_to_all(send_buf, 'ep', 0, 0, tiled=True)
        wg_full = lax.all_gather(w_gate, 'fsdp', axis=1, tiled=True)
        wu_full = lax.all_gather(w_up, 'fsdp', axis=1, tiled=True)
        wd_full = lax.all_gather(w_down, 'fsdp', axis=2, tiled=True)
        act_a = jnp.einsum('sncd,ndf->sncf', recv_buf, wg_full, preferred_element_type=jnp.float32)
        act_b = jnp.einsum('sncd,ndf->sncf', recv_buf, wu_full, preferred_element_type=jnp.float32)
        hidden = (jax.nn.silu(act_a) * act_b).astype(jnp.bfloat16)
        expert_out = jnp.einsum('sncf,nfd->sncd', hidden, wd_full, preferred_element_type=jnp.float32).astype(jnp.bfloat16)
        back_buf = lax.all_to_all(expert_out, 'ep', 0, 0, tiled=True)
        back_rows = back_buf.reshape(num_experts * capacity, model_dim)
        pair_out = jnp.einsum('tkf,fd->tkd', select, back_rows, preferred_element_type=jnp.float32)
        mixed = tokens.astype(jnp.float32) + jnp.sum(gates[:, :, None] * pair_out, axis=1)
        return mixed.astype(jnp.bfloat16)

    return jax.shard_map(device_step, mesh=mesh, in_specs=(row_spec, row_spec, row_spec, P('ep', 'fsdp', None), P('ep', 'fsdp', None), P('ep', None, 'fsdp')), out_specs=row_spec, check_vma=False)
```

profile of v0, /device:TPU:0, one launch (start us, length us, event | category | flops | bytes accessed | tf_op | source)
XLA Modules:
  0.0 528.1 jit_solution(17023513620503544047)
XLA Ops:
  6.5 0.8 copy.24
  7.4 0.1 eq.65
  7.6 0.7 broadcast_multiply_fusion
  8.4 18.1 %reduce-window.6 = s32[64,12,128]{2,1,0:T(8,128)S(1)} reduce-window(s32[64,12,128]{2,1,0:T(8,128)S(1)} %fusion.32, s32[]{:T(128)} %constant.4.clone.1), window={size=1x1x128 pad=0_0x0_0x127_0}, to_apply=%region_0.0 | reduce-window | flops 12484608 | bytes 786436 | tf_op jit(solution)/shard_map/reduce-window
  26.5 0.2 slice.8
  26.7 0.3 copy.26
  27.1 0.2 broadcast_add_fusion
  27.3 0.2 fusion.35
  27.5 0.1 reduce_sum.30
  27.9 2.9 convert_reduce_fusion
  30.9 7.7 %fusion.37 = bf16[3072,2048]{1,0:T(8,128)(2,1)} fusion(bf16[256,3072]{1,0:T(8,128)(2,1)S(1)} %convert_reduce_fusion, bf16[256,2048]{1,0:T(8,128)(2,1)} %param.6), kind=kOutput, calls=%fused_computation.39 | convolution fusion | flops 3221225472 | bytes 15204352 | tf_op jit(solution)/shard_map/tkf,td->fd/dot_general | solution.py:29
  38.5 11.8 %all-to-all-start = ((bf16[64,1,48,2048]{3,2,1,0:T(8,128)(2,1)}), bf16[64,1,48,2048]{3,2,1,0:T(8,128)(2,1)}, u32[]{:S(2)}, u32[]{:S(2)}) async-start(bf16[64,1,48,2048]{3,2,1,0:T(8,128)(2,1)} %bitcast.127), calls=%async_computation | async-start | bytes 25165824 | tf_op jit(solution)/shard_map/all_to_all | solution.py:31
  50.4 0.7 all-gather.6.cloned.1.call-update
  51.1 0.7 all-gather.4.cloned.1.call-update
  51.8 0.2 all-gather.8.cloned.1.call-start
  52.1 0.5 all-gather.8.cloned.1.call-update
  52.6 20.7 %all-gather.6.cloned.1.call-done = bf16[1,2048,1408]{2,1,0:T(8,128)(2,1)} async-done(((bf16[1,1024,1408]{2,1,0:T(8,128)(2,1)}), bf16[1,2048,1408]{2,1,0:T(8,128)(2,1)}) %all-gather.6.cloned.1.call-update) | async-done | bytes 5767184 | tf_op jit(solution)/shard_map/all_gather | solution.py:33
  73.3 179.7 %all-to-all-done = bf16[64,1,48,2048]{3,2,1,0:T(8,128)(2,1)} async-done(((bf16[64,1,48,2048]{3,2,1,0:T(8,128)(2,1)}), bf16[64,1,48,2048]{3,2,1,0:T(8,128)(2,1)}, u32[]{:S(2)}, u32[]{:S(2)}) %all-to-all-start) | async-done | bytes 12582944 | tf_op jit(solution)/shard_map/all_to_all | solution.py:31
  253.1 25.7 %fusion.8 = f32[64,48,1408]{2,1,0:T(8,128)} fusion(bf16[64,1,48,2048]{3,2,1,0:T(8,128)(2,1)} %all-to-all-done, bf16[1,2048,1408]{2,1,0:T(8,128)(2,1)} %all-gather.6.cloned.1.call-done), kind=kOutput, calls=%fused_computation.13 | convolution fusion | flops 17716740096 | bytes 35651584 | tf_op jit(solution)/shard_map/sncd,ndf->sncf/dot_general | solution.py:36
  278.8 28.3 %fusion.50 = bf16[64,48,1408]{2,1,0:T(8,128)(2,1)} fusion(f32[64,48,1408]{2,1,0:T(8,128)} %fusion.8, bf16[64,1,48,2048]{3,2,1,0:T(8,128)(2,1)} %all-to-all-done, bf16[1,2048,1408]{2,1,0:T(8,128)(2,1)} %all-gather.4.cloned.1.call-done), kind=kOutput, calls=%fused_computation.22.clone.clone.clone.1 | convolution fusion | flops 17742692352 | bytes 44302336 | tf_op jit(solution)/shard_map/sncd,ndf->sncf/dot_general | solution.py:35
  307.1 23.5 %convert_bitcast_fusion = bf16[64,1,48,2048]{3,2,1,0:T(8,128)(2,1)S(1)} fusion(bf16[1,1408,2048]{2,1,0:T(8,128)(2,1)} %all-gather.8.cloned.1.call-done, bf16[64,48,1408]{2,1,0:T(8,128)(2,1)} %fusion.50), kind=kOutput, calls=%fused_computation.18 | convolution fusion | flops 17723031552 | bytes 27000832 | tf_op jit(solution)/shard_map/sncf,nfd->sncd/dot_general | solution.py:38
  330.6 168.3 %all_to_all.10 = bf16[64,1,48,2048]{3,2,1,0:T(8,128)(2,1)S(1)} all-to-all(bf16[64,1,48,2048]{3,2,1,0:T(8,128)(2,1)S(1)} %convert_bitcast_fusion), channel_id=1, replica_groups=mesh['rep'=1,'fsdp'=2,'ep'=64] {'ep'}, dimensions={0} | all-to-all | bytes 25165824 | tf_op jit(solution)/shard_map/all_to_all | solution.py:39
  498.9 21.3 %multiply_reduce_fusion = f32[256,2048]{1,0:T(8,128)S(1)} fusion(f32[256,6]{0,1:T(8,128)S(1)} %copy-done.1, bf16[3072,2048,1]{1,0,2:T(8,128)(2,1)S(1)} %bitcast.128, s32[256,6]{0,1:T(8,128)S(1)} %copy.30), kind=kOutput, calls=%fused_computation.17 | convolution fusion | flops 19337838592 | bytes 14692352 | tf_op jit(solution)/shard_map/tkf,fd->tkd/dot_general | solution.py:41
  520.2 1.3 add_convert_fusion
  (15 shorter events, 0.6 us)
Async XLA Ops:
  38.5 214.5 %all-to-all-start = ((bf16[64,1,48,2048]{3,2,1,0:T(8,128)(2,1)}), bf16[64,1,48,2048]{3,2,1,0:T(8,128)(2,1)}, u32[]{:S(2)}, u32[]{:S(2)}) async-start(bf16[64,1,48,2048]{3,2,1,0:T(8,128)(2,1)} %bitcast.127), calls=%async_computation | async-start | bytes 25165824 | tf_op jit(solution)/shard_map/all_to_all | solution.py:31
  50.3 23.0 %all-gather.6.cloned.1.call-start = ((), (), s32[]{:S(2)}) async-start(), calls=%async_computation.3 | async-start | bytes 8650752 | tf_op jit(solution)/shard_map/all_gather | solution.py:33
  51.1 227.7 %all-gather.4.cloned.1.call-start = ((), (), s32[]{:S(2)}) async-start(), calls=%async_computation.2 | async-start | bytes 8650752 | tf_op jit(solution)/shard_map/all_gather | solution.py:32
  51.8 255.3 %all-gather.8.cloned.1.call-start = ((), (), s32[]{:S(2)}) async-start(), calls=%async_computation.4 | async-start | bytes 8650752 | tf_op jit(solution)/shard_map/all_gather | solution.py:34
  330.6 168.3 %copy-start.1 = (f32[256,6]{0,1:T(8,128)S(1)}, f32[256,6]{0,1:T(8,128)}, u32[]{:S(2)}) copy-start(f32[256,6]{0,1:T(8,128)} %param.8) | copy-start | bytes 18436
  498.9 21.3 %copy-start = (bf16[256,2048]{1,0:T(8,128)(2,1)S(1)}, bf16[256,2048]{1,0:T(8,128)(2,1)}, u32[]{:S(2)}) copy-start(bf16[256,2048]{1,0:T(8,128)(2,1)} %param.6) | copy-start | bytes 3145732
Sparse Core Ops, SparseCore 0:
  52.8 20.4 all-gather.5
  74.9 20.5 all-gather.3
  97.2 20.5 all-gather.7
where the time goes:
time: 532 us; the launch traced here: 528 us
  waiting for transfers between devices  202 us (38%)
  blocking collectives  168 us (32%)
  matrix products  107 us (20%)
  other arithmetic  23.6 us (4%)
  between operations  13.2 us (2%)
  starting transfers between devices  12.1 us (2%)
    all_to_all x1, waiting for transfers between devices, device_step(): recv_buf = lax.all_to_all(send_buf, 'ep', 0, 0, tiled=True)  180 us
    all_to_all x1, blocking collectives, device_step(): back_buf = lax.all_to_all(expert_out, 'ep', 0, 0, tiled=True)  168 us
    dot_general x1, matrix products, device_step(): jnp.einsum('sncd,ndf->sncf', recv_buf, wg_full, preferred_element_type=jn...  28.3 us
    dot_general x1, matrix products, device_step(): jnp.einsum('sncd,ndf->sncf', recv_buf, wu_full, preferred_element_type=jn...  25.7 us
    dot_general x1, matrix products, device_step(): jnp.einsum('sncf,nfd->sncd', hidden, wd_full, preferred_element_type=jnp....  23.5 us
    dot_general x1, matrix products, device_step(): jnp.einsum('tkf,fd->tkd', select, back_rows, preferred_element_type=jnp.f...  21.3 us
    all_gather x1, waiting for transfers between devices, device_step(): wu_full = lax.all_gather(w_up, 'fsdp', axis=1, tiled=True)  20.7 us
    another operation x3, other arithmetic  18.4 us
  transfers between devices with their start and end apart: 4, of which 2 were waited for; matrix products, arithmetic and copies ran while one was open for 10% of the time, Pallas kernels for 0%

commit v1 on v0

v1 whole, which is shorter than its diff:
```python
import functools

import jax
import jax.numpy as jnp
from jax import lax
from jax.experimental import pallas as pl
from jax.experimental.pallas import tpu as pltpu
from jax.sharding import PartitionSpec as P

F32 = jnp.float32
BF16 = jnp.bfloat16
VMEM_LIMIT = 60 * 1024 * 1024


def expert_rows(idx_t, n_exp):
    tok = idx_t.shape[1]
    eid = lax.broadcasted_iota(jnp.int32, (n_exp, tok), 0)
    hit = jnp.zeros((n_exp, tok), F32)
    for j in range(idx_t.shape[0]):
        hit = jnp.where(idx_t[j:j + 1, :] == eid, 1.0, hit)
    return hit, eid


def slot_keys(hit):
    tok = hit.shape[1]
    src = lax.broadcasted_iota(jnp.int32, (tok, tok), 0)
    dst = lax.broadcasted_iota(jnp.int32, (tok, tok), 1)
    earlier = jnp.where(src < dst, 1.0, 0.0).astype(BF16)
    before = jnp.dot(hit.astype(BF16), earlier, preferred_element_type=F32)
    return jnp.where(hit > 0.5, before, -1.0)


def send_kernel(base, width, group, idx_ref, tok_ref, out_ref, key_ref):
    @pl.when(pl.program_id(0) == 0)
    def _():
        hit, _ = expert_rows(idx_ref[...], key_ref.shape[0])
        key_ref[...] = slot_keys(hit)

    keys = key_ref[pl.ds(pl.program_id(0) * group, group), :]
    slot = lax.broadcasted_iota(jnp.int32, (width, keys.shape[1]), 0).astype(F32) + float(base)
    pick = [jnp.where(keys[g:g + 1, :] == slot, 1.0, 0.0) for g in range(group)]
    pick = jnp.concatenate(pick, axis=0).astype(BF16)
    out_ref[...] = jnp.dot(pick, tok_ref[...], preferred_element_type=F32).astype(BF16)


def build_send(idx_t, tokens, n_exp, base, width):
    tok, dim = tokens.shape
    group = 8
    rows = n_exp * width
    return pl.pallas_call(
        functools.partial(send_kernel, base, width, group),
        grid=(n_exp // group,),
        out_shape=jax.ShapeDtypeStruct((rows, dim), BF16),
        in_specs=[pl.BlockSpec((idx_t.shape[0], tok), lambda i: (0, 0)), pl.BlockSpec((tok, dim), lambda i: (0, 0))],
        out_specs=pl.BlockSpec((group * width, dim), lambda i: (i, 0)),
        scratch_shapes=[pltpu.VMEM((n_exp, tok), F32)],
        compiler_params=pltpu.CompilerParams(dimension_semantics=("arbitrary",), vmem_limit_bytes=VMEM_LIMIT),
        cost_estimate=pl.CostEstimate(flops=2 * rows * tok * dim, bytes_accessed=2 * rows * dim, transcendentals=0),
        name="build_send",
    )(idx_t, tokens)


def mix_weight_kernel(base, width, idx_ref, gate_ref, out_ref):
    tok = idx_ref.shape[1]
    rows = out_ref.shape[1]
    n_exp = rows // width
    idx_t, gate_t = idx_ref[...], gate_ref[...]
    hit, eid = expert_rows(idx_t, n_exp)
    key = slot_keys(hit).astype(BF16)
    gate = jnp.zeros((n_exp, tok), F32)
    for j in range(idx_t.shape[0]):
        gate = jnp.where(idx_t[j:j + 1, :] == eid, gate_t[j:j + 1, :], gate)
    col = lax.broadcasted_iota(jnp.int32, (n_exp, rows), 1)
    own = lax.broadcasted_iota(jnp.int32, (n_exp, rows), 0) * width
    spread = jnp.where((col >= own) & (col < own + width), 1.0, 0.0).astype(BF16)
    slot = jnp.sum(jnp.where((col >= own) & (col < own + width), (col - own).astype(F32), 0.0), axis=0, keepdims=True)
    turn = functools.partial(lax.dot_general, dimension_numbers=(((0,), (0,)), ((), ())), preferred_element_type=F32)
    mine = turn(key, spread) == slot + float(base)
    rest = gate
    for part in range(3):
        piece = rest.astype(BF16)
        rest = rest - piece.astype(F32)
        out_ref[part * tok:(part + 1) * tok, :] = jnp.where(mine, turn(piece, spread), 0.0).astype(BF16)


def build_mix(idx_t, gates_t, n_exp, base, width):
    tok = idx_t.shape[1]
    return pl.pallas_call(
        functools.partial(mix_weight_kernel, base, width),
        out_shape=jax.ShapeDtypeStruct((3 * tok, n_exp * width), BF16),
        compiler_params=pltpu.CompilerParams(vmem_limit_bytes=VMEM_LIMIT),
        cost_estimate=pl.CostEstimate(flops=8 * tok * n_exp * n_exp * width, bytes_accessed=6 * tok * n_exp * width, transcendentals=0),
        name="build_mix",
    )(idx_t, gates_t)


def ffn_kernel(x_ref, g0, g1, u0, u1, d0, d1, out_ref, wgu, wd, sems):
    half, ffn = g0.shape

    @pl.when(pl.program_id(0) == 0)
    def _():
        me = lax.axis_index('fsdp')
        copies = []
        for other, (g, u, d) in enumerate(((g0, u0, d0), (g1, u1, d1))):
            pos = me if other == 0 else 1 - me
            at = pl.ds(pl.multiple_of(pos * half, half), half)
            copies.append(pltpu.make_async_copy(g, wgu.at[at, pl.ds(0, ffn)], sems.at[other, 0]))
            copies.append(pltpu.make_async_copy(u, wgu.at[at, pl.ds(ffn, ffn)], sems.at[other, 1]))
            copies.append(pltpu.make_async_copy(d, wd.at[:, at], sems.at[other, 2]))
        for c in copies:
            c.start()
        for c in copies:
            c.wait()

    both = jnp.dot(x_ref[...], wgu[...], preferred_element_type=F32)
    act_a, act_b = both[:, :ffn], both[:, ffn:]
    hidden = (act_a * jax.nn.sigmoid(act_a) * act_b).astype(BF16)
    out_ref[...] = jnp.dot(hidden, wd[...], preferred_element_type=F32).astype(BF16)


def ffn(x, own, other):
    rows, dim = x.shape
    half, width = own[0].shape
    block = min(512, rows)
    any_spec = pl.BlockSpec(memory_space=pl.ANY)
    return pl.pallas_call(
        ffn_kernel,
        grid=(rows // block,),
        out_shape=jax.ShapeDtypeStruct((rows, dim), BF16),
        in_specs=[pl.BlockSpec((block, dim), lambda i: (i, 0))] + [any_spec] * 6,
        out_specs=pl.BlockSpec((block, dim), lambda i: (i, 0)),
        scratch_shapes=[pltpu.VMEM((dim, 2 * width), BF16), pltpu.VMEM((width, dim), BF16), pltpu.SemaphoreType.DMA((2, 3))],
        compiler_params=pltpu.CompilerParams(dimension_semantics=("arbitrary",), vmem_limit_bytes=VMEM_LIMIT),
        cost_estimate=pl.CostEstimate(flops=6 * rows * dim * width, bytes_accessed=4 * rows * dim + 6 * dim * width, transcendentals=rows * width),
        name="ffn",
    )(x, own[0], other[0], own[1], other[1], own[2], other[2])


def mix_kernel(w_ref, back_ref, base_ref, out_ref):
    tok = base_ref.shape[0]
    parts = jnp.dot(w_ref[...], back_ref[...], preferred_element_type=F32)
    total = base_ref[...].astype(F32) + (parts[:tok] + parts[tok:2 * tok] + parts[2 * tok:])
    out_ref[...] = total.astype(out_ref.dtype)


def mix(weights, back, base, dtype):
    tok, dim = base.shape
    rows = back.shape[0]
    block = min(512, dim)
    return pl.pallas_call(
        mix_kernel,
        grid=(dim // block,),
        out_shape=jax.ShapeDtypeStruct((tok, dim), dtype),
        in_specs=[pl.BlockSpec(weights.shape, lambda i: (0, 0)), pl.BlockSpec((rows, block), lambda i: (0, i)), pl.BlockSpec((tok, block), lambda i: (0, i))],
        out_specs=pl.BlockSpec((tok, block), lambda i: (0, i)),
        compiler_params=pltpu.CompilerParams(dimension_semantics=("arbitrary",), vmem_limit_bytes=VMEM_LIMIT),
        cost_estimate=pl.CostEstimate(flops=6 * tok * rows * dim, bytes_accessed=2 * rows * dim, transcendentals=0),
        name="mix",
    )(weights, back, base)


def solution(mesh):
    ep_size = mesh.shape['ep']
    row_spec = P(('rep', 'ep', 'fsdp'), None)
    swap = [(0, 1), (1, 0)]

    def device_step(tokens, expert_idx, gates, w_gate, w_up, w_down):
        tok_count, top_k = expert_idx.shape
        dim = tokens.shape[1]
        n_exp = ep_size
        capacity = (2 * tok_count * top_k + n_exp - 1) // n_exp
        width = capacity // 2
        own = (w_gate[0], w_up[0], w_down[0])
        other = tuple(lax.ppermute(w, 'fsdp', swap) for w in own)
        idx_t, gates_t = expert_idx.T, gates.T

        send_a = build_send(idx_t, tokens, n_exp, 0, width)
        send_b = build_send(idx_t, tokens, n_exp, width, width)

        def exchange(x):
            return lax.all_to_all(x.reshape(n_exp, width, dim), 'ep', 0, 0, tiled=True).reshape(n_exp * width, dim)

        in_a = exchange(send_a)
        in_b = exchange(send_b)
        mix_a = build_mix(idx_t, gates_t, n_exp, 0, width)
        mix_b = build_mix(idx_t, gates_t, n_exp, width, width)
        out_a = ffn(in_a, own, other)
        back_a = exchange(out_a)
        out_b = ffn(in_b, own, other)
        back_b = exchange(out_b)
        part = mix(mix_a, back_a, tokens, F32)
        return mix(mix_b, back_b, part, BF16)

    return jax.shard_map(device_step, mesh=mesh, in_specs=(row_spec, row_spec, row_spec, P('ep', 'fsdp', None), P('ep', 'fsdp', None), P('ep', None, 'fsdp')), out_specs=row_spec, check_vma=False)
```

time: 532 us -> 425 us (0.80)
  blocking collectives: 168 us -> 0 us
  Pallas kernels: 0 us -> 120 us
  matrix products: 107 us -> 0 us
  waiting for transfers between devices: 202 us -> 249 us
  starting transfers between devices: 12.1 us -> 48 us
  other arithmetic: 23.6 us -> 0 us
  between operations: 13.2 us -> 0.07 us
    all_to_all x1 -> x0, blocking collectives: 168 us -> none  [device_step(): back_buf = lax.all_to_all(expert_out, 'ep', 0, 0, tiled=True)]
    pallas_call x0 -> x8, Pallas kernels: none -> 120 us  [the longest x2 81.1 us: ffn(): pl.pallas_call(ffn_kernel, grid=(rows // block,), out_shape=jax.ShapeDtyp...]
    dot_general x5 -> x0, matrix products: 107 us -> none  [the longest x1 28.3 us: device_step(): jnp.einsum('sncd,ndf->sncf', recv_buf, wg_full, preferred_element_type=jn...]
    all_to_all x1 -> x4, waiting for transfers between devices: 180 us -> 239 us  [exchange(): lax.all_to_all(x.reshape(n_exp, width, dim), 'ep', 0, 0, tiled=True)]
    all_to_all x1 -> x4, starting transfers between devices: 11.8 us -> 46.9 us  [exchange(): lax.all_to_all(x.reshape(n_exp, width, dim), 'ep', 0, 0, tiled=True)]
    all_gather x3 -> x0, waiting for transfers between devices: 20.7 us -> none  [the longest x1 20.7 us: device_step(): wu_full = lax.all_gather(w_up, 'fsdp', axis=1, tiled=True)]
    another operation x3 -> x0, other arithmetic: 18.4 us -> none
    ppermute x0 -> x3, waiting for transfers between devices: none -> 9.34 us  [device_step(): other = tuple((lax.ppermute(w, 'fsdp', swap) for w in own))]
  transfers between devices with their start and end apart: 4 -> 7, of which waited for: 2 -> 7; matrix products, arithmetic and copies ran while one was open for 10% -> 0% of each run, Pallas kernels for 0% -> 25%
where the time goes in v1:
time: 425 us; the launch traced here: 421 us
  waiting for transfers between devices  249 us (59%)
  Pallas kernels  120 us (28%)
  starting transfers between devices  48 us (11%)
  local copies, waits for them, and re-layouts  4.86 us (1%)
    all_to_all x4, waiting for transfers between devices, exchange(): lax.all_to_all(x.reshape(n_exp, width, dim), 'ep', 0, 0, tiled=True)  239 us
    pallas_call x2, Pallas kernels, ffn(): pl.pallas_call(ffn_kernel, grid=(rows // block,), out_shape=jax.ShapeDtyp...  81.1 us
    all_to_all x4, starting transfers between devices, exchange(): lax.all_to_all(x.reshape(n_exp, width, dim), 'ep', 0, 0, tiled=True)  46.9 us
    pallas_call x2, Pallas kernels, mix(): pl.pallas_call(mix_kernel, grid=(dim // block,), out_shape=jax.ShapeDtype...  17.8 us
    pallas_call x2, Pallas kernels, build_send(): pl.pallas_call(functools.partial(send_kernel, base, width, group), grid=(...  14.1 us
    ppermute x3, waiting for transfers between devices, device_step(): other = tuple((lax.ppermute(w, 'fsdp', swap) for w in own))  9.34 us
  transfers between devices with their start and end apart: 7, of which 7 were waited for; matrix products, arithmetic and copies ran while one was open for 0% of the time, Pallas kernels for 25%

profile of v1, /device:TPU:0, one launch (start us, length us, event | category | flops | bytes accessed | tf_op | source)
XLA Modules:
  0.0 421.5 jit_solution(1920579222186098712)
XLA Ops:
  0.0 7.0 %build_send.3 = bf16[1536,2048]{1,0:T(8,128)(2,1)} custom-call(s32[6,256]{1,0:T(8,128)} %bitcast.17, bf16[256,2048]{1,0:T(8,128)(2,1)} %base_ref.1), custom_call_target="tpu_custom_call" | custom-call | flops 1610612736 | bytes 6291456 | tf_op jit(solution)/shard_map/build_send/pallas_call | solution.py:50
  7.0 11.8 %all-to-all-start.2 = ((bf16[64,24,2048]{2,1,0:T(8,128)(2,1)}), bf16[64,24,2048]{2,1,0:T(8,128)(2,1)}, u32[]{:S(2)}, u32[]{:S(2)}) async-start(bf16[64,24,2048]{2,1,0:T(8,128)(2,1)} %bitcast.14), calls=%async_computation.2 | async-start | bytes 12582912 | tf_op jit(solution)/shard_map/all_to_all | solution.py:181
  18.8 7.1 %build_send.2 = bf16[1536,2048]{1,0:T(8,128)(2,1)} custom-call(s32[6,256]{1,0:T(8,128)} %bitcast.18, bf16[256,2048]{1,0:T(8,128)(2,1)} %base_ref.1), custom_call_target="tpu_custom_call" | custom-call | flops 1610612736 | bytes 6291456 | tf_op jit(solution)/shard_map/build_send/pallas_call | solution.py:50
  25.8 89.1 %all-to-all-done.2 = bf16[64,24,2048]{2,1,0:T(8,128)(2,1)} async-done(((bf16[64,24,2048]{2,1,0:T(8,128)(2,1)}), bf16[64,24,2048]{2,1,0:T(8,128)(2,1)}, u32[]{:S(2)}, u32[]{:S(2)}) %all-to-all-start.2) | async-done | bytes 6291488 | tf_op jit(solution)/shard_map/all_to_all | solution.py:181
  115.0 6.9 %all-to-all-start = ((bf16[64,24,2048]{2,1,0:T(8,128)(2,1)}), bf16[64,24,2048]{2,1,0:T(8,128)(2,1)}, u32[]{:S(2)}, u32[]{:S(2)}) async-start(bf16[64,24,2048]{2,1,0:T(8,128)(2,1)} %bitcast.13), calls=%async_computation | async-start | bytes 12582912 | tf_op jit(solution)/shard_map/all_to_all | solution.py:181
  121.9 0.6 collective-permute-start
  122.6 0.4 collective-permute-start.2
  123.0 4.4 %collective-permute-done.g1 = bf16[1024,1408]{1,0:T(8,128)(2,1)S(1)} collective-permute-done((bf16[1024,1408]{1,0:T(8,128)(2,1)S(1)}, bf16[1024,1408]{1,0:T(8,128)(2,1)S(1)}, u32[]{:S(2)}, u32[]{:S(2)}) %collective-permute-start) | collective-permute-done | bytes 2883616 | tf_op jit(solution)/shard_map/ppermute | solution.py:174
  127.4 1.7 copy-done.1
  129.1 2.5 collective-permute-done.1.u1
  131.5 1.6 copy-done.2
  133.2 2.5 collective-permute-done.2.d1
  135.7 1.5 copy-done.3
  137.2 40.5 %ffn.3 = bf16[1536,2048]{1,0:T(8,128)(2,1)} custom-call(bf16[1536,2048]{1,0:T(8,128)(2,1)} %bitcast.10.x_ref, bf16[1024,1408]{1,0:T(8,128)(2,1)} %bitcast.23, bf16[1024,1408]{1,0:T(8,128)(2,1)} %copy-done.1, bf16[1024,1408]{1,0:T(8,128)(2,1)} %bitcast.27, bf16[1024,1408]{1,0:T(8,128)(2,1)} %copy-done.2, bf16[1408,1024]{1,0:T(8,128)(2,1)} %bitcast.30, ...), custom_call_target="tpu_custom_call" | custom-call | flops 26575110144 | bytes 29884416 | tf_op jit(solution)/shard_map/ffn/pallas_call | solution.py:126
  177.8 33.4 %all-to-all-done = bf16[64,24,2048]{2,1,0:T(8,128)(2,1)} async-done(((bf16[64,24,2048]{2,1,0:T(8,128)(2,1)}), bf16[64,24,2048]{2,1,0:T(8,128)(2,1)}, u32[]{:S(2)}, u32[]{:S(2)}) %all-to-all-start) | async-done | bytes 6291488 | tf_op jit(solution)/shard_map/all_to_all | solution.py:181
  211.2 18.4 %all-to-all-start.3 = ((bf16[64,24,2048]{2,1,0:T(8,128)(2,1)}), bf16[64,24,2048]{2,1,0:T(8,128)(2,1)}, u32[]{:S(2)}, u32[]{:S(2)}) async-start(bf16[64,24,2048]{2,1,0:T(8,128)(2,1)} %bitcast.16), calls=%async_computation.3 | async-start | bytes 12582912 | tf_op jit(solution)/shard_map/all_to_all | solution.py:181
  229.6 40.6 %ffn.2 = bf16[1536,2048]{1,0:T(8,128)(2,1)} custom-call(bf16[1536,2048]{1,0:T(8,128)(2,1)} %bitcast.3.x_ref, bf16[1024,1408]{1,0:T(8,128)(2,1)} %bitcast.24, bf16[1024,1408]{1,0:T(8,128)(2,1)} %copy-done.1, bf16[1024,1408]{1,0:T(8,128)(2,1)} %bitcast.28, bf16[1024,1408]{1,0:T(8,128)(2,1)} %copy-done.2, bf16[1408,1024]{1,0:T(8,128)(2,1)} %bitcast.31, ...), custom_call_target="tpu_custom_call" | custom-call | flops 26575110144 | bytes 29884416 | tf_op jit(solution)/shard_map/ffn/pallas_call | solution.py:126
  270.2 43.1 %all-to-all-done.3 = bf16[64,24,2048]{2,1,0:T(8,128)(2,1)} async-done(((bf16[64,24,2048]{2,1,0:T(8,128)(2,1)}), bf16[64,24,2048]{2,1,0:T(8,128)(2,1)}, u32[]{:S(2)}, u32[]{:S(2)}) %all-to-all-start.3) | async-done | bytes 6291488 | tf_op jit(solution)/shard_map/all_to_all | solution.py:181
  313.3 9.8 %all-to-all-start.1 = ((bf16[64,24,2048]{2,1,0:T(8,128)(2,1)}), bf16[64,24,2048]{2,1,0:T(8,128)(2,1)}, u32[]{:S(2)}, u32[]{:S(2)}) async-start(bf16[64,24,2048]{2,1,0:T(8,128)(2,1)} %bitcast.15), calls=%async_computation.1 | async-start | bytes 12582912 | tf_op jit(solution)/shard_map/all_to_all | solution.py:181
  323.1 3.4 build_mix.3.w_ref
  326.5 3.4 build_mix.2.w_ref
  329.9 9.0 %mix.2.base_ref = f32[256,2048]{1,0:T(8,128)} custom-call(bf16[768,1536]{1,0:T(8,128)(2,1)} %build_mix.3.w_ref, bf16[1536,2048]{1,0:T(8,128)(2,1)} %bitcast.12.back_ref, bf16[256,2048]{1,0:T(8,128)(2,1)} %base_ref.1), custom_call_target="tpu_custom_call" | custom-call | flops 4831838208 | bytes 6291456 | tf_op jit(solution)/shard_map/mix/pallas_call | solution.py:150
  338.8 73.7 %all-to-all-done.1 = bf16[64,24,2048]{2,1,0:T(8,128)(2,1)} async-done(((bf16[64,24,2048]{2,1,0:T(8,128)(2,1)}), bf16[64,24,2048]{2,1,0:T(8,128)(2,1)}, u32[]{:S(2)}, u32[]{:S(2)}) %all-to-all-start.1) | async-done | bytes 6291488 | tf_op jit(solution)/shard_map/all_to_all | solution.py:181
  412.6 8.9 %mix.3 = bf16[256,2048]{1,0:T(8,128)(2,1)} custom-call(bf16[768,1536]{1,0:T(8,128)(2,1)} %build_mix.2.w_ref, bf16[1536,2048]{1,0:T(8,128)(2,1)} %bitcast.8.back_ref, f32[256,2048]{1,0:T(8,128)} %mix.2.base_ref), custom_call_target="tpu_custom_call" | custom-call | flops 4831838208 | bytes 6291456 | tf_op jit(solution)/shard_map/mix/pallas_call | solution.py:150
  (6 shorter events, 0.1 us)
Async XLA Ops:
  7.0 108.0 %all-to-all-start.2 = ((bf16[64,24,2048]{2,1,0:T(8,128)(2,1)}), bf16[64,24,2048]{2,1,0:T(8,128)(2,1)}, u32[]{:S(2)}, u32[]{:S(2)}) async-start(bf16[64,24,2048]{2,1,0:T(8,128)(2,1)} %bitcast.14), calls=%async_computation.2 | async-start | bytes 12582912 | tf_op jit(solution)/shard_map/all_to_all | solution.py:181
  115.0 6.9 %copy-start = (bf16[1,1024,1408]{2,1,0:T(8,128)(2,1)S(1)}, bf16[1,1024,1408]{2,1,0:T(8,128)(2,1)}, u32[]{:S(2)}) copy-start(bf16[1,1024,1408]{2,1,0:T(8,128)(2,1)} %param.9) | copy-start | bytes 8650756
  115.0 96.2 %all-to-all-start = ((bf16[64,24,2048]{2,1,0:T(8,128)(2,1)}), bf16[64,24,2048]{2,1,0:T(8,128)(2,1)}, u32[]{:S(2)}, u32[]{:S(2)}) async-start(bf16[64,24,2048]{2,1,0:T(8,128)(2,1)} %bitcast.13), calls=%async_computation | async-start | bytes 12582912 | tf_op jit(solution)/shard_map/all_to_all | solution.py:181
  121.9 5.5 %collective-permute-start = (bf16[1024,1408]{1,0:T(8,128)(2,1)S(1)}, bf16[1024,1408]{1,0:T(8,128)(2,1)S(1)}, u32[]{:S(2)}, u32[]{:S(2)}) collective-permute-start(bf16[1024,1408]{1,0:T(8,128)(2,1)S(1)} %bitcast.25), channel_id=1, source_target_pairs={{0,64},{64,0},{1,65},{65,1},{2,66},{66,2},{3,67},{67,3},{4,68},{68... | collective-permute-start | bytes 8650760 | tf_op jit(solution)/shard_map/ppermute | solution.py:174
  122.5 9.0 %collective-permute-start.1 = (bf16[1024,1408]{1,0:T(8,128)(2,1)}, bf16[1024,1408]{1,0:T(8,128)(2,1)S(1)}, u32[]{:S(2)}, u32[]{:S(2)}) collective-permute-start(bf16[1024,1408]{1,0:T(8,128)(2,1)} %bitcast.26), channel_id=1, source_target_pairs={{0,64},{64,0},{1,65},{65,1},{2,66},{66,2},{3,67},{67,3},{4,68},{68... | collective-permute-start | bytes 8650760 | tf_op jit(solution)/shard_map/ppermute | solution.py:174
  122.6 13.1 %collective-permute-start.2 = (bf16[1408,1024]{1,0:T(8,128)(2,1)}, bf16[1408,1024]{1,0:T(8,128)(2,1)S(1)}, u32[]{:S(2)}, u32[]{:S(2)}) collective-permute-start(bf16[1408,1024]{1,0:T(8,128)(2,1)} %bitcast.29), channel_id=1, source_target_pairs={{0,64},{64,0},{1,65},{65,1},{2,66},{66,2},{3,67},{67,3},{4,68},{68... | collective-permute-start | bytes 8650760 | tf_op jit(solution)/shard_map/ppermute | solution.py:174
  127.4 1.7 copy-start.1
  131.5 1.6 copy-start.2
  135.7 1.6 copy-start.3
  211.2 102.0 %all-to-all-start.3 = ((bf16[64,24,2048]{2,1,0:T(8,128)(2,1)}), bf16[64,24,2048]{2,1,0:T(8,128)(2,1)}, u32[]{:S(2)}, u32[]{:S(2)}) async-start(bf16[64,24,2048]{2,1,0:T(8,128)(2,1)} %bitcast.16), calls=%async_computation.3 | async-start | bytes 12582912 | tf_op jit(solution)/shard_map/all_to_all | solution.py:181
  313.3 99.3 %all-to-all-start.1 = ((bf16[64,24,2048]{2,1,0:T(8,128)(2,1)}), bf16[64,24,2048]{2,1,0:T(8,128)(2,1)}, u32[]{:S(2)}, u32[]{:S(2)}) async-start(bf16[64,24,2048]{2,1,0:T(8,128)(2,1)} %bitcast.15), calls=%async_computation.1 | async-start | bytes 12582912 | tf_op jit(solution)/shard_map/all_to_all | solution.py:181

commit v2 on v0

v2 whole, which is shorter than its diff:
```python
import functools

import jax
import jax.numpy as jnp
from jax import lax
from jax.experimental import pallas as pl
from jax.experimental.pallas import tpu as pltpu
from jax.sharding import PartitionSpec as P

F32 = jnp.float32
BF16 = jnp.bfloat16
MESH = pl.DeviceIdType.MESH
SIDE = 4
STRIDE = (16, 4, 1)
N_EXP = 64
GROUPS, PER = 8, 8
RING = 4


def hits(idx_t, eid):
    hit = jnp.zeros((eid.shape[0], idx_t.shape[1]), F32)
    for j in range(6):
        hit = jnp.where(idx_t[j:j + 1, :] == eid, 1.0, hit)
    return hit


def slot_keys(hit, earlier):
    before = jnp.dot(hit.astype(BF16), earlier, preferred_element_type=F32)
    return jnp.where(hit > 0.5, before, -1.0)


def offset(g, i):
    dz = i // 2
    dy = (i % 2) * 2 + lax.rem(g, 2)
    dx = lax.rem(dz + dy + lax.div(g, 2), SIDE)
    return dz, dy, dx


def layer_kernel(cap, cuts, idx_ref, gate_ref, tok_ref, wg, wu, wd, out_ref, recv, back,
                 wgu, wdn, toks_z, toks_y, toks_x, idx_all, mixw, acc,
                 ag_send, ag_recv, ix_send, ix_recv, d_send, d_recv, w_loc, w_send, w_recv, c_send, c_recv):
    tok, dim = tok_ref.shape
    half, ffn = wg.shape
    rows = PER * cap
    me = lax.axis_index('ep')
    core = lax.axis_index('fsdp')
    pos = (lax.div(me, 16), lax.rem(lax.div(me, 4), 4), lax.rem(me, 4))
    gathered = (toks_z, toks_y, toks_x)

    def shifted(a, k):
        return me + (lax.rem(pos[a] + k, SIDE) - pos[a]) * STRIDE[a]

    def ag_copies(a, k):
        dev = {'ep': shifted(a, k)}
        lo, hi = cuts[a], cuts[a + 1]
        yield pltpu.make_async_remote_copy(src_ref=idx_ref, dst_ref=idx_all.at[a, k - 1], send_sem=ix_send.at[a, k - 1],
                                           recv_sem=ix_recv.at[a, k - 1], device_id=dev, device_id_type=MESH)
        yield pltpu.make_async_remote_copy(src_ref=tok_ref.at[:, pl.ds(lo, hi - lo)], dst_ref=gathered[a].at[k - 1],
                                           send_sem=ag_send.at[a, k - 1], recv_sem=ag_recv.at[a, k - 1],
                                           device_id=dev, device_id_type=MESH)

    for k in (2, 1, 3):
        for a in range(3):
            for c in ag_copies(a, k):
                c.start()

    at = pl.ds(pl.multiple_of(core * half, half), half)
    spots = ((wg, wgu.at[at, pl.ds(0, ffn)]), (wu, wgu.at[at, pl.ds(ffn, ffn)]), (wd, wdn.at[:, at]))
    w_copies = []
    for n, (src, dst) in enumerate(spots):
        w_copies.append(pltpu.make_async_copy(src, dst, w_loc.at[n]))
        w_copies.append(pltpu.make_async_remote_copy(src_ref=src, dst_ref=dst, send_sem=w_send.at[n], recv_sem=w_recv.at[n],
                                                     device_id={'fsdp': 1 - core}, device_id_type=MESH))
    for c in w_copies:
        c.start()

    before = lax.broadcasted_iota(jnp.int32, (tok, tok), 0)
    after = lax.broadcasted_iota(jnp.int32, (tok, tok), 1)
    earlier = jnp.where(before < after, 1.0, 0.0).astype(BF16)
    slot = lax.broadcasted_iota(jnp.int32, (cap, tok), 0).astype(F32)

    def plane_ids(a):
        q = lax.broadcasted_iota(jnp.int32, (16, 1), 0)
        u, v = q >> 2, q & 3
        others = [b for b in range(3) if b != a]
        first = ((pos[others[0]] + u) & 3) * STRIDE[others[0]]
        second = ((pos[others[1]] + v) & 3) * STRIDE[others[1]]
        return first + second + pos[a] * STRIDE[a]

    def place(a, lo, hi):
        spot = [slice(None) if b == a else pos[b] for b in range(3)]
        return recv.at[spot[0], spot[1], spot[2], :, pl.ds(lo, hi - lo)]

    def plane_copies(a, stage):
        lo, hi = cuts[a], cuts[a + 1]
        others = [b for b in range(3) if b != a]
        yield pltpu.make_async_copy(stage.at[0], place(a, lo, hi), d_send.at[a, 0])
        for q in (10, 5, 15, 7, 13, 2, 8, 6, 9, 11, 14, 1, 4, 3, 12):
            dev = me
            for b, step in zip(others, (q // 4, q % 4)):
                dev = dev + (lax.rem(pos[b] + step, SIDE) - pos[b]) * STRIDE[b]
            yield pltpu.make_async_remote_copy(src_ref=stage.at[q], dst_ref=place(a, lo, hi), send_sem=d_send.at[a, q],
                                               recv_sem=d_recv.at[a, q], device_id={'ep': dev}, device_id_type=MESH)

    def dispatch(stage_z, stage_y, stage_x):
        stages = (stage_z, stage_y, stage_x)

        def pick(a, k):
            lo, hi = cuts[a], cuts[a + 1]
            if k == 0:
                ids, block = idx_ref[...], tok_ref[:, lo:hi]
            else:
                for c in ag_copies(a, k):
                    c.wait_recv()
                ids, block = idx_all[a, k - 1], gathered[a][k - 1]
            key = slot_keys(hits(ids, plane_ids(a)), earlier)
            sel = [jnp.where(key[q:q + 1, :] == slot, 1.0, 0.0) for q in range(16)]
            sel = jnp.concatenate(sel, axis=0).astype(BF16)
            got = jnp.dot(sel, block, preferred_element_type=F32).astype(BF16)
            line = lax.rem(pos[a] + SIDE - k, SIDE)
            for q in range(16):
                stages[a][q, line] = got[q * cap:(q + 1) * cap]

        for a in range(3):
            pick(a, 0)
        for a in range(3):
            for k in (1, 3, 2):
                pick(a, k)
            for c in plane_copies(a, stages[a]):
                c.start()
        for a in range(3):
            for k in (2, 1, 3):
                for c in ag_copies(a, k):
                    c.wait_send()
        build_mix()
        for c in w_copies:
            c.wait()
        for a in range(3):
            for n, c in enumerate(plane_copies(a, stages[a])):
                if n == 0:
                    c.wait()
                else:
                    c.wait_recv()
                    c.wait_send()

    def build_mix():
        idx_t, gate_t = idx_ref[...], gate_ref[...]
        eid = lax.broadcasted_iota(jnp.int32, (N_EXP, tok), 0)
        key = slot_keys(hits(idx_t, eid), earlier).astype(BF16)
        gate = jnp.zeros((N_EXP, tok), F32)
        for j in range(6):
            gate = jnp.where(idx_t[j:j + 1, :] == eid, gate_t[j:j + 1, :], gate)
        pieces = []
        left = gate
        for part in range(3):
            pieces.append(left.astype(BF16))
            left = left - pieces[-1].astype(F32)
        turn = functools.partial(lax.dot_general, dimension_numbers=(((0,), (0,)), ((), ())), preferred_element_type=F32)
        col = lax.broadcasted_iota(jnp.int32, (N_EXP, rows), 1)
        row = lax.broadcasted_iota(jnp.int32, (N_EXP, rows), 0)
        nth = jnp.zeros((N_EXP, rows), jnp.int32)
        for n in range(1, PER):
            nth = nth + jnp.where(col >= n * cap, 1, 0)
        want = (col - nth * cap)[0:1].astype(F32)
        dz = nth >> 1

        @pl.loop(0, GROUPS)
        def _(g):
            dy = (nth & 1) * 2 + lax.rem(g, 2)
            dx = (dz + dy + lax.div(g, 2)) & 3
            exp = ((pos[0] - dz) & 3) * 16 + ((pos[1] - dy) & 3) * 4 + ((pos[2] - dx) & 3)
            spread = jnp.where(exp == row, 1.0, 0.0).astype(BF16)
            mine = turn(key, spread) == want
            span = pl.ds(pl.multiple_of(g * rows, 128), rows)
            for part in range(3):
                mixw[part * tok:(part + 1) * tok, span] = jnp.where(mine, turn(pieces[part], spread), 0.0).astype(BF16)

    stage_types = [pltpu.VMEM((16, SIDE, cap, cuts[a + 1] - cuts[a]), BF16) for a in range(3)]
    pl.run_scoped(dispatch, *stage_types)

    def work(xbuf, outs, land, x_sem, m_sem):
        def loads(g, do):
            for i in range(PER):
                dz, dy, dx = offset(g, i)
                src = recv.at[lax.rem(pos[0] + dz, SIDE), lax.rem(pos[1] + dy, SIDE), lax.rem(pos[2] + dx, SIDE)]
                pltpu.make_async_copy(src, xbuf.at[lax.rem(g, 2), pl.ds(i * cap, cap)], x_sem.at[lax.rem(g, 2)]).start()

        def sends(g):
            ring = lax.rem(g, RING)
            for i in range(PER):
                dz, dy, dx = offset(g, i)
                dev = lax.rem(pos[0] + dz, SIDE) * 16 + lax.rem(pos[1] + dy, SIDE) * 4 + lax.rem(pos[2] + dx, SIDE)
                span = pl.ds(i * cap, cap)

                def far():
                    pltpu.make_async_remote_copy(src_ref=outs.at[ring, span], dst_ref=back.at[g, span], send_sem=c_send.at[ring],
                                                 recv_sem=c_recv.at[g], device_id={'ep': dev}, device_id_type=MESH).start()

                if i > 0:
                    far()
                else:
                    pl.when(g > 0)(far)

                    @pl.when(g == 0)
                    def _():
                        pltpu.make_async_copy(outs.at[ring, span], back.at[g, span], c_send.at[ring]).start()

        def drain(ring):
            pltpu.make_async_copy(outs.at[ring], outs.at[ring], c_send.at[ring]).wait()

        loads(0, None)

        @pl.loop(0, GROUPS)
        def _(g):
            now = lax.rem(g, 2)
            pltpu.make_async_copy(xbuf.at[now], xbuf.at[now], x_sem.at[now]).wait()

            @pl.when(g < GROUPS - 1)
            def _():
                loads(g + 1, None)

            @pl.when(g >= RING)
            def _():
                drain(lax.rem(g, RING))

            both = jnp.dot(xbuf[now], wgu[...], preferred_element_type=F32)
            act_a, act_b = both[:, :ffn], both[:, ffn:]
            hidden = (act_a * jax.nn.sigmoid(act_a) * act_b).astype(BF16)
            outs[lax.rem(g, RING)] = jnp.dot(hidden, wdn[...], preferred_element_type=F32).astype(BF16)
            sends(g)

        for ring in range(RING):
            drain(ring)
        acc[...] = tok_ref[...].astype(F32)

        @pl.loop(0, GROUPS // 2)
        def _(r):
            for s in range(2):
                g = 2 * r + s

                @pl.when(g == 0)
                def _():
                    part = back.at[0, pl.ds(cap, rows - cap)]
                    pltpu.make_async_copy(part, part, c_recv.at[0]).wait()

                @pl.when(g > 0)
                def _():
                    pltpu.make_async_copy(back.at[g], back.at[g], c_recv.at[g]).wait()

            pltpu.make_async_copy(back.at[pl.ds(2 * r, 2)], land, m_sem).start()
            pltpu.make_async_copy(back.at[pl.ds(2 * r, 2)], land, m_sem).wait()
            w = mixw[:, pl.ds(pl.multiple_of(r * 2 * rows, 128), 2 * rows)]
            for n in range(0, dim, 512):
                block = land[:, :, n:n + 512].reshape(2 * rows, 512)
                parts = jnp.dot(w, block, preferred_element_type=F32)
                acc[:, n:n + 512] += parts[:tok] + parts[tok:2 * tok] + parts[2 * tok:]

        out_ref[...] = acc[...].astype(BF16)

    pl.run_scoped(work, pltpu.VMEM((2, rows, dim), BF16), pltpu.VMEM((RING, rows, dim), BF16), pltpu.VMEM((2, rows, dim), BF16),
                  pltpu.SemaphoreType.DMA((2,)), pltpu.SemaphoreType.DMA)


def solution(mesh):
    row_spec = P(('rep', 'ep', 'fsdp'), None)

    def device_step(tokens, expert_idx, gates, w_gate, w_up, w_down):
        tok, top_k = expert_idx.shape
        dim = tokens.shape[1]
        half, width = w_gate.shape[1:]
        cap = (2 * tok * top_k + N_EXP - 1) // N_EXP
        cuts = (0, 640, 1280, dim)
        rows = PER * cap
        idx_t = jnp.pad(expert_idx.T, ((0, 8 - top_k), (0, 0)))
        gate_t = gates.T
        vmem = pl.BlockSpec(memory_space=pltpu.VMEM)
        hbm = pl.BlockSpec(memory_space=pl.ANY)
        sem = pltpu.SemaphoreType.DMA
        out, _, _ = pl.pallas_call(
            functools.partial(layer_kernel, cap, cuts),
            out_shape=(jax.ShapeDtypeStruct((tok, dim), BF16), jax.ShapeDtypeStruct((SIDE, SIDE, SIDE, cap, dim), BF16),
                       jax.ShapeDtypeStruct((GROUPS, rows, dim), BF16)),
            in_specs=[vmem, vmem, vmem, hbm, hbm, hbm],
            out_specs=(vmem, hbm, hbm),
            scratch_shapes=[pltpu.VMEM((dim, 2 * width), BF16), pltpu.VMEM((width, dim), BF16)]
            + [pltpu.VMEM((3, tok, cuts[a + 1] - cuts[a]), BF16) for a in range(3)]
            + [pltpu.VMEM((3, 3, 8, tok), jnp.int32), pltpu.VMEM((3 * tok, N_EXP * cap), BF16), pltpu.VMEM((tok, dim), F32),
               sem((3, 3)), sem((3, 3)), sem((3, 3)), sem((3, 3)), sem((3, 16)), sem((3, 16)), sem((3,)), sem((3,)), sem((3,)),
               sem((RING,)), sem((GROUPS,))],
            compiler_params=pltpu.CompilerParams(has_side_effects=True, vmem_limit_bytes=63 * 1024 * 1024),
            name="moe_layer",
        )(idx_t, gate_t, tokens, w_gate[0], w_up[0], w_down[0])
        return out

    return jax.shard_map(device_step, mesh=mesh, in_specs=(row_spec, row_spec, row_spec, P('ep', 'fsdp', None), P('ep', 'fsdp', None), P('ep', None, 'fsdp')), out_specs=row_spec, check_vma=False)
```

time: 532 us -> 390 us (0.73)
  the two profiles are of different devices: /device:TPU:0 before, /device:TPU:68 now
where the time goes in v2:
time: 390 us
  Pallas kernels  386 us (99%)
    pallas_call x1, Pallas kernels, device_step(): pl.pallas_call(functools.partial(layer_kernel, cap, cuts), out_shape=(jax...  386 us

profile of v2, /device:TPU:68, one launch (start us, length us, event | category | flops | bytes accessed | tf_op | source)
XLA Modules:
  0.0 389.6 jit_solution(113214354487718934)
XLA Ops:
  0.0 1.3 pad.4.idx_ref
  1.3 385.9 %moe_layer.1 = (bf16[256,2048]{1,0:T(8,128)(2,1)}, bf16[4,4,4,48,2048]{4,3,2,1,0:T(8,128)(2,1)}, bf16[8,384,2048]{2,1,0:T(8,128)(2,1)}) custom-call(s32[8,256]{1,0:T(8,128)} %pad.4.idx_ref, f32[6,256]{1,0:T(8,128)} %bitcast.8, bf16[256,2048]{1,0:T(8,128)(2,1)} %tok_ref.1, bf16[1024,1408]{1,0:T(8,128)(2,1)} %bitcast.5, bf16[1024,1408]{1,0:T(8,128)(2,1)} %bitcast.6, ...), custom_call_target="tpu_custom_call" | custom-call | tf_op jit(solution)/shard_map/moe_layer/pallas_call | solution.py:279
  387.3 2.3 copy.8

commit v3 on v2

--- a/solution.py
+++ b/solution.py
@@ -14,6 +14,7 @@
 STRIDE = (16, 4, 1)
 N_EXP = 64
 GROUPS, PER = 8, 8
+ROUTES = ((2, 1, 0), (1, 0, 2), (0, 2, 1))
 RING = 4
 
 
@@ -30,15 +31,27 @@
 
 
 def offset(g, i):
-    dz = i // 2
-    dy = (i % 2) * 2 + lax.rem(g, 2)
-    dx = lax.rem(dz + dy + lax.div(g, 2), SIDE)
-    return dz, dy, dx
+    dz, b = i // 2, i % 2
+    lean = 2 * b + lax.rem(g, 2)
+    return dz, lax.rem(dz + lean, SIDE), lax.rem(lean + lax.div(g, 2) + SIDE - dz, SIDE)
+
+
+def moved(d):
+    return (d + SIDE - 1) // SIDE if isinstance(d, int) else lax.div(d + SIDE - 1, SIDE)
+
+
+def if_moves(d, far, near=None):
+    if isinstance(d, int):
+        (far if d else near or (lambda: None))()
+        return
+    pl.when(d > 0)(far)
+    if near is not None:
+        pl.when(d == 0)(near)
 
 
 def layer_kernel(cap, cuts, idx_ref, gate_ref, tok_ref, wg, wu, wd, out_ref, recv, back,
                  wgu, wdn, toks_z, toks_y, toks_x, idx_all, mixw, acc,
-                 ag_send, ag_recv, ix_send, ix_recv, d_send, d_recv, w_loc, w_send, w_recv, c_send, c_recv):
+                 ag_send, ag_recv, ix_send, ix_recv, d_send, d_recv, w_loc, w_send, w_recv, c_send, c_keep, c_recv, r_send):
     tok, dim = tok_ref.shape
     half, ffn = wg.shape
     rows = PER * cap
@@ -71,9 +84,6 @@
         w_copies.append(pltpu.make_async_copy(src, dst, w_loc.at[n]))
         w_copies.append(pltpu.make_async_remote_copy(src_ref=src, dst_ref=dst, send_sem=w_send.at[n], recv_sem=w_recv.at[n],
                                                      device_id={'fsdp': 1 - core}, device_id_type=MESH))
-    for c in w_copies:
-        c.start()
-
     before = lax.broadcasted_iota(jnp.int32, (tok, tok), 0)
     after = lax.broadcasted_iota(jnp.int32, (tok, tok), 1)
     earlier = jnp.where(before < after, 1.0, 0.0).astype(BF16)
@@ -121,13 +131,14 @@
             for q in range(16):
                 stages[a][q, line] = got[q * cap:(q + 1) * cap]
 
-        for a in range(3):
-            pick(a, 0)
-        for a in range(3):
-            for k in (1, 3, 2):
+        for k in (0, 1, 3, 2):
+            for a in range(3):
                 pick(a, k)
-            for c in plane_copies(a, stages[a]):
+        for trio in zip(*(plane_copies(a, stages[a]) for a in range(3))):
+            for c in trio:
                 c.start()
+        for c in w_copies:
+            c.start()
         for a in range(3):
             for k in (2, 1, 3):
                 for c in ag_copies(a, k):
@@ -166,8 +177,9 @@
 
         @pl.loop(0, GROUPS)
         def _(g):
-            dy = (nth & 1) * 2 + lax.rem(g, 2)
-            dx = (dz + dy + lax.div(g, 2)) & 3
+            lean = (nth & 1) * 2 + lax.rem(g, 2)
+            dy = (dz + lean) & 3
+            dx = (lean + lax.div(g, 2) - dz) & 3
             exp = ((pos[0] - dz) & 3) * 16 + ((pos[1] - dy) & 3) * 4 + ((pos[2] - dx) & 3)
             spread = jnp.where(exp == row, 1.0, 0.0).astype(BF16)
             mine = turn(key, spread) == want
@@ -179,45 +191,61 @@
     pl.run_scoped(dispatch, *stage_types)
 
     def work(xbuf, outs, land, x_sem, m_sem):
-        def loads(g, do):
+        def loads(g):
             for i in range(PER):
                 dz, dy, dx = offset(g, i)
                 src = recv.at[lax.rem(pos[0] + dz, SIDE), lax.rem(pos[1] + dy, SIDE), lax.rem(pos[2] + dx, SIDE)]
                 pltpu.make_async_copy(src, xbuf.at[lax.rem(g, 2), pl.ds(i * cap, cap)], x_sem.at[lax.rem(g, 2)]).start()
 
-        def sends(g):
+        def block(i, p):
+            return pl.ds(i * cap, cap), pl.ds(cuts[p], cuts[p + 1] - cuts[p])
+
+        def hop(src, stage, g, i, p, d, send):
+            axis = ROUTES[p][stage]
+            return pltpu.make_async_remote_copy(
+                src_ref=src, dst_ref=back.at[stage, g, *block(i, p)], send_sem=send, recv_sem=c_recv.at[stage, g],
+                device_id={'ep': shifted(axis, d)}, device_id_type=MESH)
+
+        def each(g):
+            for i in range(PER):
+                ds = offset(g, i)
+                for p in range(3):
+                    yield i, p, [ds[axis] for axis in ROUTES[p]]
+
+        def first_hops(g):
             ring = lax.rem(g, RING)
-            for i in range(PER):
-                dz, dy, dx = offset(g, i)
-                dev = lax.rem(pos[0] + dz, SIDE) * 16 + lax.rem(pos[1] + dy, SIDE) * 4 + lax.rem(pos[2] + dx, SIDE)
-                span = pl.ds(i * cap, cap)
-
-                def far():
-                    pltpu.make_async_remote_copy(src_ref=outs.at[ring, span], dst_ref=back.at[g, span], send_sem=c_send.at[ring],
-                                                 recv_sem=c_recv.at[g], device_id={'ep': dev}, device_id_type=MESH).start()
-
-                if i > 0:
-                    far()
-                else:
-                    pl.when(g > 0)(far)
-
-                    @pl.when(g == 0)
-                    def _():
-                        pltpu.make_async_copy(outs.at[ring, span], back.at[g, span], c_send.at[ring]).start()
+            for i, p, d in each(g):
+                src = outs.at[ring, *block(i, p)]
+                if_moves(d[0], lambda: hop(src, 0, g, i, p, d[0], c_send.at[ring]).start(),
+                         lambda: pltpu.make_async_copy(src, back.at[0, g, *block(i, p)], c_keep.at[g]).start())
+
+        def second_hops(g):
+            arrived(0, g)
+            part = back.at[0, g, pl.ds(0, rows - far)]
+            pltpu.make_async_copy(part, part, c_keep.at[g]).wait()
+            for i, p, d in each(g):
+                if_moves(d[1], lambda: hop(back.at[0, g, *block(i, p)], 1, g, i, p, d[1], r_send.at[0]).start())
+
+        def third_hops(g):
+            arrived(1, g)
+            for i, p, d in each(g):
+                if_moves(d[2], lambda: hop(back.at[moved(d[1]), g, *block(i, p)], 2, g, i, p, d[2], r_send.at[1]).start())
+
+        def arrived(stage, g):
+            part = back.at[stage, g, pl.ds(0, far)]
+            pltpu.make_async_copy(part, part, c_recv.at[stage, g]).wait()
 
         def drain(ring):
-            pltpu.make_async_copy(outs.at[ring], outs.at[ring], c_send.at[ring]).wait()
-
-        loads(0, None)
-
-        @pl.loop(0, GROUPS)
-        def _(g):
+            part = outs.at[ring, pl.ds(0, far)]
+            pltpu.make_async_copy(part, part, c_send.at[ring]).wait()
+
+        def experts(g):
             now = lax.rem(g, 2)
             pltpu.make_async_copy(xbuf.at[now], xbuf.at[now], x_sem.at[now]).wait()
 
             @pl.when(g < GROUPS - 1)
             def _():
-                loads(g + 1, None)
+                loads(g + 1)
 
             @pl.when(g >= RING)
             def _():
@@ -227,37 +255,50 @@
             act_a, act_b = both[:, :ffn], both[:, ffn:]
             hidden = (act_a * jax.nn.sigmoid(act_a) * act_b).astype(BF16)
             outs[lax.rem(g, RING)] = jnp.dot(hidden, wdn[...], preferred_element_type=F32).astype(BF16)
-            sends(g)
-
+            first_hops(g)
+
+        def mix(g):
+            arrived(2, g)
+            for i, p, d in each(g):
+                last = moved(d[2])
+                stage = 2 * last + (1 - last) * moved(d[1])
+                pltpu.make_async_copy(back.at[stage, g, *block(i, p)], land.at[block(i, p)], m_sem).start()
+            pltpu.make_async_copy(land, land, m_sem).wait()
+            w = mixw[:, pl.ds(pl.multiple_of(g * rows, 128), rows)]
+            for n in range(0, dim, 512):
+                parts = jnp.dot(w, land[:, n:n + 512], preferred_element_type=F32)
+                acc[:, n:n + 512] += parts[:tok] + parts[tok:2 * tok] + parts[2 * tok:]
+
+        far = rows // SIDE * (SIDE - 1)
+        acc[...] = tok_ref[...].astype(F32)
+        loads(0)
+
+        @pl.loop(0, GROUPS + 3)
+        def _(r):
+            @pl.when(r < GROUPS)
+            def _():
+                experts(r)
+
+            @pl.when((r >= 1) & (r < GROUPS + 1))
+            def _():
+                second_hops(r - 1)
+
+            @pl.when((r >= 2) & (r < GROUPS + 2))
+            def _():
+                third_hops(r - 2)
+
+            @pl.when(r >= 3)
+            def _():
+                mix(r - 3)
+
+        out_ref[...] = acc[...].astype(BF16)
         for ring in range(RING):
             drain(ring)
-        acc[...] = tok_ref[...].astype(F32)
-
-        @pl.loop(0, GROUPS // 2)
-        def _(r):
-            for s in range(2):
-                g = 2 * r + s
-
-                @pl.when(g == 0)
-                def _():
-                    part = back.at[0, pl.ds(cap, rows - cap)]
-                    pltpu.make_async_copy(part, part, c_recv.at[0]).wait()
-
-                @pl.when(g > 0)
-                def _():
-                    pltpu.make_async_copy(back.at[g], back.at[g], c_recv.at[g]).wait()
-
-            pltpu.make_async_copy(back.at[pl.ds(2 * r, 2)], land, m_sem).start()
-            pltpu.make_async_copy(back.at[pl.ds(2 * r, 2)], land, m_sem).wait()
-            w = mixw[:, pl.ds(pl.multiple_of(r * 2 * rows, 128), 2 * rows)]
-            for n in range(0, dim, 512):
-                block = land[:, :, n:n + 512].reshape(2 * rows, 512)
-                parts = jnp.dot(w, block, preferred_element_type=F32)
-                acc[:, n:n + 512] += parts[:tok] + parts[tok:2 * tok] + parts[2 * tok:]
-
-        out_ref[...] = acc[...].astype(BF16)
-
-    pl.run_scoped(work, pltpu.VMEM((2, rows, dim), BF16), pltpu.VMEM((RING, rows, dim), BF16), pltpu.VMEM((2, rows, dim), BF16),
+        for n in range(2):
+            part = back.at[0, :, pl.ds(0, far)]
+            pltpu.make_async_copy(part, part, r_send.at[n]).wait()
+
+    pl.run_scoped(work, pltpu.VMEM((2, rows, dim), BF16), pltpu.VMEM((RING, rows, dim), BF16), pltpu.VMEM((rows, dim), BF16),
                   pltpu.SemaphoreType.DMA((2,)), pltpu.SemaphoreType.DMA)
 
 
@@ -279,14 +320,14 @@
         out, _, _ = pl.pallas_call(
             functools.partial(layer_kernel, cap, cuts),
             out_shape=(jax.ShapeDtypeStruct((tok, dim), BF16), jax.ShapeDtypeStruct((SIDE, SIDE, SIDE, cap, dim), BF16),
-                       jax.ShapeDtypeStruct((GROUPS, rows, dim), BF16)),
+                       jax.ShapeDtypeStruct((3, GROUPS, rows, dim), BF16)),
             in_specs=[vmem, vmem, vmem, hbm, hbm, hbm],
             out_specs=(vmem, hbm, hbm),
             scratch_shapes=[pltpu.VMEM((dim, 2 * width), BF16), pltpu.VMEM((width, dim), BF16)]
             + [pltpu.VMEM((3, tok, cuts[a + 1] - cuts[a]), BF16) for a in range(3)]
             + [pltpu.VMEM((3, 3, 8, tok), jnp.int32), pltpu.VMEM((3 * tok, N_EXP * cap), BF16), pltpu.VMEM((tok, dim), F32),
                sem((3, 3)), sem((3, 3)), sem((3, 3)), sem((3, 3)), sem((3, 16)), sem((3, 16)), sem((3,)), sem((3,)), sem((3,)),
-               sem((RING,)), sem((GROUPS,))],
+               sem((RING,)), sem((GROUPS,)), sem((3, GROUPS)), sem((2,))],
             compiler_params=pltpu.CompilerParams(has_side_effects=True, vmem_limit_bytes=63 * 1024 * 1024),
             name="moe_layer",
         )(idx_t, gate_t, tokens, w_gate[0], w_up[0], w_down[0])

time: 390 us -> 321 us (0.82)
  the two profiles are of different devices: /device:TPU:68 before, /device:TPU:0 now
where the time goes in v3:
time: 321 us; the launch traced here: 318 us
  Pallas kernels  314 us (98%)
  local copies, waits for them, and re-layouts  3.6 us (1%)
    pallas_call x1, Pallas kernels, device_step(): pl.pallas_call(functools.partial(layer_kernel, cap, cuts), out_shape=(jax...  314 us

profile of v3, /device:TPU:0, one launch (start us, length us, event | category | flops | bytes accessed | tf_op | source)
XLA Modules:
  0.0 318.1 jit_solution(10148896605230155403)
XLA Ops:
  0.0 1.3 pad.4.idx_ref
  1.3 314.5 %moe_layer.1 = (bf16[256,2048]{1,0:T(8,128)(2,1)}, bf16[4,4,4,48,2048]{4,3,2,1,0:T(8,128)(2,1)}, bf16[3,8,384,2048]{3,2,1,0:T(8,128)(2,1)}) custom-call(s32[8,256]{1,0:T(8,128)} %pad.4.idx_ref, f32[6,256]{1,0:T(8,128)} %bitcast.8, bf16[256,2048]{1,0:T(8,128)(2,1)} %tok_ref.1, bf16[1024,1408]{1,0:T(8,128)(2,1)} %bitcast.5, bf16[1024,1408]{1,0:T(8,128)(2,1)} %bitcast.6, ...), custom_call_target="tpu_custom_call" | custom-call | tf_op jit(solution)/shard_map/moe_layer/pallas_call | solution.py:320
  315.8 2.3 copy.8

commit v4 on v0

v4 whole, which is shorter than its diff:
```python
import functools

import jax
import jax.numpy as jnp
from jax import lax
from jax.experimental import pallas as pl
from jax.experimental.pallas import tpu as pltpu
from jax.sharding import PartitionSpec as P

F32 = jnp.float32
BF16 = jnp.bfloat16
MESH = pl.DeviceIdType.MESH
SIDE = 4
STRIDE = (16, 4, 1)
N_EXP = 64
GROUPS, PER = 8, 8
ROUTES = ((2, 1, 0), (1, 0, 2), (0, 2, 1))
OUT_ROUTES = ((0, 1, 2), (1, 2, 0), (2, 0, 1))
LEAD = 2
RING = 4


def hits(idx_t, eid):
    hit = jnp.zeros((eid.shape[0], idx_t.shape[1]), F32)
    for j in range(6):
        hit = jnp.where(idx_t[j:j + 1, :] == eid, 1.0, hit)
    return hit


def slot_keys(hit, earlier):
    before = jnp.dot(hit.astype(BF16), earlier, preferred_element_type=F32)
    return jnp.where(hit > 0.5, before, -1.0)


def offset(g, i):
    dz, b = i // 2, i % 2
    lean = 2 * b + lax.rem(g, 2)
    return dz, lax.rem(dz + lean, SIDE), lax.rem(lean + lax.div(g, 2) + SIDE - dz, SIDE)


def moved(d):
    return (d + SIDE - 1) // SIDE if isinstance(d, int) else lax.div(d + SIDE - 1, SIDE)


def if_moves(d, far, near=None):
    if isinstance(d, int):
        (far if d else near or (lambda: None))()
        return
    pl.when(d > 0)(far)
    if near is not None:
        pl.when(d == 0)(near)


def layer_kernel(cap, cuts, idx_ref, gate_ref, tok_ref, wg, wu, wd, out_ref, inbox, back,
                 wgu, wdn, toks_z, toks_y, toks_x, idx_all, keys, mixw, acc, stage, xbuf, outs, land,
                 ag_send, ag_recv, ix_send, ix_recv, w_loc, w_send, w_recv,
                 d_send, d_keep, d_recv, d_relay, c_send, c_keep, c_recv, c_relay, x_sem, m_sem):
    tok, dim = tok_ref.shape
    half, ffn = wg.shape
    rows = PER * cap
    far = rows // SIDE * (SIDE - 1)
    me = lax.axis_index('ep')
    core = lax.axis_index('fsdp')
    pos = (lax.div(me, 16), lax.rem(lax.div(me, 4), 4), lax.rem(me, 4))
    gathered = (toks_z, toks_y, toks_x)

    def shifted(a, k):
        return me + (lax.rem(pos[a] + k, SIDE) - pos[a]) * STRIDE[a]

    def ag_copies(a, k):
        dev = {'ep': shifted(a, k)}
        lo, hi = cuts[a], cuts[a + 1]
        yield pltpu.make_async_remote_copy(src_ref=idx_ref, dst_ref=idx_all.at[a, k - 1], send_sem=ix_send.at[a, k - 1],
                                           recv_sem=ix_recv.at[a, k - 1], device_id=dev, device_id_type=MESH)
        yield pltpu.make_async_remote_copy(src_ref=tok_ref.at[:, pl.ds(lo, hi - lo)], dst_ref=gathered[a].at[k],
                                           send_sem=ag_send.at[a, k - 1], recv_sem=ag_recv.at[a, k - 1],
                                           device_id=dev, device_id_type=MESH)

    for k in (2, 1, 3):
        for a in range(3):
            for c in ag_copies(a, k):
                c.start()

    at = pl.ds(pl.multiple_of(core * half, half), half)
    spots = ((wg, wgu.at[at, pl.ds(0, ffn)]), (wu, wgu.at[at, pl.ds(ffn, ffn)]), (wd, wdn.at[:, at]))
    w_copies = []
    for n, (src, dst) in enumerate(spots):
        w_copies.append(pltpu.make_async_copy(src, dst, w_loc.at[n]))
        w_copies.append(pltpu.make_async_remote_copy(src_ref=src, dst_ref=dst, send_sem=w_send.at[n], recv_sem=w_recv.at[n],
                                                     device_id={'fsdp': 1 - core}, device_id_type=MESH))

    before = lax.broadcasted_iota(jnp.int32, (tok, tok), 0)
    after = lax.broadcasted_iota(jnp.int32, (tok, tok), 1)
    earlier = jnp.where(before < after, 1.0, 0.0).astype(BF16)
    slot = lax.broadcasted_iota(jnp.int32, (cap, tok), 0).astype(F32)

    def block(i, p):
        return pl.ds(i * cap, cap), pl.ds(cuts[p], cuts[p + 1] - cuts[p])

    def each(g, routes):
        for i in range(PER):
            ds = offset(g, i)
            for p in range(3):
                yield i, p, [ds[axis] for axis in routes[p]]

    def wait_rows(ref, n, sem):
        part = ref.at[pl.ds(0, n)]
        pltpu.make_async_copy(part, part, sem).wait()

    def plane_keys(a, k):
        q = lax.broadcasted_iota(jnp.int32, (16, 1), 0)
        _, b, c = OUT_ROUTES[a]
        eid = pos[a] * STRIDE[a] + ((pos[b] + (q >> 2)) & 3) * STRIDE[b] + ((pos[c] + (q & 3)) & 3) * STRIDE[c]
        ids = idx_ref[...] if k == 0 else idx_all[a, k - 1]
        keys[a, k] = slot_keys(hits(ids, eid), earlier)

    def back_of(d):
        return (SIDE - d) % SIDE if isinstance(d, int) else lax.rem(SIDE - d, SIDE)

    def pick(g):
        ring = lax.rem(g, RING)

        @pl.when(g >= RING)
        def _():
            wait_rows(stage.at[ring], far, d_send.at[ring])

        for i, p, d in each(g, OUT_ROUTES):
            lo, hi = cuts[p], cuts[p + 1]
            k = back_of(d[0])
            key = keys[p, k, pl.ds(back_of(d[1]) * 4 + back_of(d[2]), 1), :]
            sel = jnp.where(key == slot, 1.0, 0.0).astype(BF16)
            got = jnp.dot(sel, gathered[p][k], preferred_element_type=F32)
            stage[ring, i * cap:(i + 1) * cap, lo:hi] = got.astype(BF16)
        for i, p, d in each(g, OUT_ROUTES):
            src, dst = stage.at[ring, *block(i, p)], inbox.at[0, g, *block(i, p)]
            if_moves(d[1], lambda: pltpu.make_async_remote_copy(
                src_ref=src, dst_ref=dst, send_sem=d_send.at[ring], recv_sem=d_recv.at[0, g],
                device_id={'ep': shifted(OUT_ROUTES[p][1], back_of(d[1]))}, device_id_type=MESH).start(),
                lambda: pltpu.make_async_copy(src, dst, d_keep.at[g]).start())

    def forward(g):
        wait_rows(inbox.at[0, g], far, d_recv.at[0, g])
        wait_rows(inbox.at[0, g], rows - far, d_keep.at[g])
        for i, p, d in each(g, OUT_ROUTES):
            if_moves(d[2], lambda: pltpu.make_async_remote_copy(
                src_ref=inbox.at[0, g, *block(i, p)], dst_ref=inbox.at[1, g, *block(i, p)], send_sem=d_relay,
                recv_sem=d_recv.at[1, g], device_id={'ep': shifted(OUT_ROUTES[p][2], back_of(d[2]))}, device_id_type=MESH).start())

    def fetch(g):
        wait_rows(inbox.at[1, g], far, d_recv.at[1, g])
        for i, p, d in each(g, OUT_ROUTES):
            pltpu.make_async_copy(inbox.at[moved(d[2]), g, *block(i, p)], xbuf.at[block(i, p)], x_sem).start()

    def build_mix():
        idx_t, gate_t = idx_ref[...], gate_ref[...]
        eid = lax.broadcasted_iota(jnp.int32, (N_EXP, tok), 0)
        key = slot_keys(hits(idx_t, eid), earlier).astype(BF16)
        gate = jnp.zeros((N_EXP, tok), F32)
        for j in range(6):
            gate = jnp.where(idx_t[j:j + 1, :] == eid, gate_t[j:j + 1, :], gate)
        pieces = []
        left = gate
        for part in range(3):
            pieces.append(left.astype(BF16))
            left = left - pieces[-1].astype(F32)
        turn = functools.partial(lax.dot_general, dimension_numbers=(((0,), (0,)), ((), ())), preferred_element_type=F32)
        col = lax.broadcasted_iota(jnp.int32, (N_EXP, rows), 1)
        row = lax.broadcasted_iota(jnp.int32, (N_EXP, rows), 0)
        nth = jnp.zeros((N_EXP, rows), jnp.int32)
        for n in range(1, PER):
            nth = nth + jnp.where(col >= n * cap, 1, 0)
        want = (col - nth * cap)[0:1].astype(F32)
        dz = nth >> 1

        @pl.loop(0, GROUPS)
        def _(g):
            lean = (nth & 1) * 2 + lax.rem(g, 2)
            dy = (dz + lean) & 3
            dx = (lean + lax.div(g, 2) - dz) & 3
            exp = ((pos[0] - dz) & 3) * 16 + ((pos[1] - dy) & 3) * 4 + ((pos[2] - dx) & 3)
            spread = jnp.where(exp == row, 1.0, 0.0).astype(BF16)
            mine = turn(key, spread) == want
            span = pl.ds(pl.multiple_of(g * rows, 128), rows)
            for part in range(3):
                mixw[part * tok:(part + 1) * tok, span] = jnp.where(mine, turn(pieces[part], spread), 0.0).astype(BF16)

    def experts(g):
        ring = lax.rem(g, RING)
        pltpu.make_async_copy(xbuf, xbuf, x_sem).wait()

        @pl.when(g >= RING)
        def _():
            wait_rows(outs.at[ring], far, c_send.at[ring])

        both = jnp.dot(xbuf[...], wgu[...], preferred_element_type=F32)
        act_a, act_b = both[:, :ffn], both[:, ffn:]
        hidden = (act_a * jax.nn.sigmoid(act_a) * act_b).astype(BF16)
        outs[ring] = jnp.dot(hidden, wdn[...], preferred_element_type=F32).astype(BF16)
        for i, p, d in each(g, ROUTES):
            src = outs.at[ring, *block(i, p)]
            if_moves(d[0], lambda: hop(src, 0, g, i, p, d[0], c_send.at[ring]).start(),
                     lambda: pltpu.make_async_copy(src, back.at[0, g, *block(i, p)], c_keep.at[g]).start())

    def hop(src, leg, g, i, p, d, send):
        return pltpu.make_async_remote_copy(
            src_ref=src, dst_ref=back.at[leg, g, *block(i, p)], send_sem=send, recv_sem=c_recv.at[leg, g],
            device_id={'ep': shifted(ROUTES[p][leg], d)}, device_id_type=MESH)

    def second_hops(g):
        wait_rows(back.at[0, g], far, c_recv.at[0, g])
        wait_rows(back.at[0, g], rows - far, c_keep.at[g])
        for i, p, d in each(g, ROUTES):
            if_moves(d[1], lambda: hop(back.at[0, g, *block(i, p)], 1, g, i, p, d[1], c_relay.at[0]).start())

    def third_hops(g):
        wait_rows(back.at[1, g], far, c_recv.at[1, g])
        for i, p, d in each(g, ROUTES):
            if_moves(d[2], lambda: hop(back.at[moved(d[1]), g, *block(i, p)], 2, g, i, p, d[2], c_relay.at[1]).start())

    def mix(g):
        wait_rows(back.at[2, g], far, c_recv.at[2, g])
        for i, p, d in each(g, ROUTES):
            last = moved(d[2])
            leg = 2 * last + (1 - last) * moved(d[1])
            pltpu.make_async_copy(back.at[leg, g, *block(i, p)], land.at[block(i, p)], m_sem).start()
        pltpu.make_async_copy(land, land, m_sem).wait()
        w = mixw[:, pl.ds(pl.multiple_of(g * rows, 128), rows)]
        for n in range(0, dim, 512):
            parts = jnp.dot(w, land[:, n:n + 512], preferred_element_type=F32)
            acc[:, n:n + 512] += parts[:tok] + parts[tok:2 * tok] + parts[2 * tok:]

    acc[...] = tok_ref[...].astype(F32)
    for a in range(3):
        gathered[a][0] = tok_ref[:, cuts[a]:cuts[a + 1]]
        plane_keys(a, 0)
    for k in (1, 3, 2):
        for a in range(3):
            for c in ag_copies(a, k):
                c.wait_recv()
            plane_keys(a, k)
    for g in range(LEAD):
        pick(jnp.int32(g))
    for c in w_copies:
        c.start()
    build_mix()
    for a in range(3):
        for k in (2, 1, 3):
            for c in ag_copies(a, k):
                c.wait_send()

    def in_turn(r, lag, step):
        g = r - lag
        pl.when((g >= 0) & (g < GROUPS))(lambda: step(g))

    @pl.loop(0, GROUPS + 4)
    def _(r):
        @pl.when(r == 1)
        def _():
            for c in w_copies:
                c.wait()

        in_turn(r, 0, forward)
        in_turn(r, 1, fetch)
        pl.when(r + LEAD < GROUPS)(lambda: pick(r + LEAD))
        in_turn(r, 1, experts)
        in_turn(r, 2, second_hops)
        in_turn(r, 3, third_hops)
        in_turn(r, 4, mix)

    out_ref[...] = acc[...].astype(BF16)
    for ring in range(RING):
        wait_rows(stage.at[ring], far, d_send.at[ring])
        wait_rows(outs.at[ring], far, c_send.at[ring])
    for sem in (d_relay, c_relay.at[0], c_relay.at[1]):
        part = back.at[0, :, pl.ds(0, far)]
        pltpu.make_async_copy(part, part, sem).wait()


def solution(mesh):
    row_spec = P(('rep', 'ep', 'fsdp'), None)

    def device_step(tokens, expert_idx, gates, w_gate, w_up, w_down):
        tok, top_k = expert_idx.shape
        dim = tokens.shape[1]
        half, width = w_gate.shape[1:]
        cap = (2 * tok * top_k + N_EXP - 1) // N_EXP
        cuts = (0, 640, 1280, dim)
        rows = PER * cap
        idx_t = jnp.pad(expert_idx.T, ((0, 8 - top_k), (0, 0)))
        gate_t = gates.T
        vmem = pl.BlockSpec(memory_space=pltpu.VMEM)
        hbm = pl.BlockSpec(memory_space=pl.ANY)
        sem = pltpu.SemaphoreType.DMA
        out, _, _ = pl.pallas_call(
            functools.partial(layer_kernel, cap, cuts),
            out_shape=(jax.ShapeDtypeStruct((tok, dim), BF16), jax.ShapeDtypeStruct((2, GROUPS, rows, dim), BF16),
                       jax.ShapeDtypeStruct((3, GROUPS, rows, dim), BF16)),
            in_specs=[vmem, vmem, vmem, hbm, hbm, hbm],
            out_specs=(vmem, hbm, hbm),
            scratch_shapes=[pltpu.VMEM((dim, 2 * width), BF16), pltpu.VMEM((width, dim), BF16)]
            + [pltpu.VMEM((SIDE, tok, cuts[a + 1] - cuts[a]), BF16) for a in range(3)]
            + [pltpu.VMEM((3, 3, 8, tok), jnp.int32), pltpu.VMEM((3, SIDE, 16, tok), F32), pltpu.VMEM((3 * tok, N_EXP * cap), BF16),
               pltpu.VMEM((tok, dim), F32), pltpu.VMEM((RING, rows, dim), BF16), pltpu.VMEM((rows, dim), BF16),
               pltpu.VMEM((RING, rows, dim), BF16), pltpu.VMEM((rows, dim), BF16),
               sem((3, 3)), sem((3, 3)), sem((3, 3)), sem((3, 3)), sem((3,)), sem((3,)), sem((3,)),
               sem((RING,)), sem((GROUPS,)), sem((2, GROUPS)), sem,
               sem((RING,)), sem((GROUPS,)), sem((3, GROUPS)), sem((2,)), sem, sem],
            compiler_params=pltpu.CompilerParams(has_side_effects=True, vmem_limit_bytes=63 * 1024 * 1024),
            name="moe_layer",
        )(idx_t, gate_t, tokens, w_gate[0], w_up[0], w_down[0])
        return out

    return jax.shard_map(device_step, mesh=mesh, in_specs=(row_spec, row_spec, row_spec, P('ep', 'fsdp', None), P('ep', 'fsdp', None), P('ep', None, 'fsdp')), out_specs=row_spec, check_vma=False)
```

time: 532 us -> 276 us (0.52)
  Pallas kernels: 0 us -> 271 us
  waiting for transfers between devices: 202 us -> 0 us
  blocking collectives: 168 us -> 0 us
  matrix products: 107 us -> 0 us
  other arithmetic: 23.6 us -> 0 us
  between operations: 13.2 us -> 0.01 us
  starting transfers between devices: 12.1 us -> 0 us
    pallas_call x0 -> x1, Pallas kernels: none -> 271 us  [device_step(): pl.pallas_call(functools.partial(layer_kernel, cap, cuts), out_shape=(jax...]
    all_to_all x1 -> x0, waiting for transfers between devices: 180 us -> none  [device_step(): recv_buf = lax.all_to_all(send_buf, 'ep', 0, 0, tiled=True)]
    all_to_all x1 -> x0, blocking collectives: 168 us -> none  [device_step(): back_buf = lax.all_to_all(expert_out, 'ep', 0, 0, tiled=True)]
    dot_general x5 -> x0, matrix products: 107 us -> none  [the longest x1 28.3 us: device_step(): jnp.einsum('sncd,ndf->sncf', recv_buf, wg_full, preferred_element_type=jn...]
    all_gather x3 -> x0, waiting for transfers between devices: 20.7 us -> none  [the longest x1 20.7 us: device_step(): wu_full = lax.all_gather(w_up, 'fsdp', axis=1, tiled=True)]
    another operation x3 -> x0, other arithmetic: 18.4 us -> none
    all_to_all x1 -> x0, starting transfers between devices: 11.8 us -> none  [device_step(): recv_buf = lax.all_to_all(send_buf, 'ep', 0, 0, tiled=True)]
  transfers between devices with their start and end apart: 4 -> 0, of which waited for: 2 -> 0; matrix products, arithmetic and copies ran while one was open for 10% -> 0% of each run, Pallas kernels for 0% -> 0%
where the time goes in v4:
time: 276 us; the launch traced here: 275 us
  Pallas kernels  271 us (98%)
  local copies, waits for them, and re-layouts  3.6 us (1%)
    pallas_call x1, Pallas kernels, device_step(): pl.pallas_call(functools.partial(layer_kernel, cap, cuts), out_shape=(jax...  271 us

profile of v4, /device:TPU:0, one launch (start us, length us, event | category | flops | bytes accessed | tf_op | source)
XLA Modules:
  0.0 275.1 jit_solution(11990077214829596048)
XLA Ops:
  0.0 1.3 pad.4.idx_ref
  1.3 271.5 %moe_layer.1 = (bf16[256,2048]{1,0:T(8,128)(2,1)}, bf16[2,8,384,2048]{3,2,1,0:T(8,128)(2,1)}, bf16[3,8,384,2048]{3,2,1,0:T(8,128)(2,1)}) custom-call(s32[8,256]{1,0:T(8,128)} %pad.4.idx_ref, f32[6,256]{1,0:T(8,128)} %bitcast.8, bf16[256,2048]{1,0:T(8,128)(2,1)} %tok_ref.1, bf16[1024,1408]{1,0:T(8,128)(2,1)} %bitcast.5, bf16[1024,1408]{1,0:T(8,128)(2,1)} %bitcast.6, ...), custom_call_target="tpu_custom_call" | custom-call | tf_op jit(solution)/shard_map/moe_layer/pallas_call | solution.py:294
  272.8 2.3 copy.8

commit v5 on v4

--- a/solution.py
+++ b/solution.py
@@ -16,7 +16,7 @@
 GROUPS, PER = 8, 8
 ROUTES = ((2, 1, 0), (1, 0, 2), (0, 2, 1))
 OUT_ROUTES = ((0, 1, 2), (1, 2, 0), (2, 0, 1))
-LEAD = 2
+LEAD = 3
 RING = 4
 
 
@@ -53,9 +53,9 @@
 
 def layer_kernel(cap, cuts, idx_ref, gate_ref, tok_ref, wg, wu, wd, out_ref, inbox, back,
                  wgu, wdn, toks_z, toks_y, toks_x, idx_all, keys, mixw, acc, stage, xbuf, outs, land,
-                 ag_send, ag_recv, ix_send, ix_recv, w_loc, w_send, w_recv,
+                 ag_send, ag_recv, ix_send, ix_recv, own_sem, w_loc, w_send, w_recv,
                  d_send, d_keep, d_recv, d_relay, c_send, c_keep, c_recv, c_relay, x_sem, m_sem):
-    tok, dim = tok_ref.shape
+    tok, dim = acc.shape
     half, ffn = wg.shape
     rows = PER * cap
     far = rows // SIDE * (SIDE - 1)
@@ -76,10 +76,11 @@
                                            send_sem=ag_send.at[a, k - 1], recv_sem=ag_recv.at[a, k - 1],
                                            device_id=dev, device_id_type=MESH)
 
-    for k in (2, 1, 3):
-        for a in range(3):
-            for c in ag_copies(a, k):
-                c.start()
+    barrier = pltpu.get_barrier_semaphore()
+    for a in range(3):
+        for k in range(1, SIDE):
+            pl.semaphore_signal(barrier, inc=1, device_id={'ep': shifted(a, k)}, device_id_type=MESH)
+    pl.semaphore_signal(barrier, inc=1, device_id={'fsdp': 1 - core}, device_id_type=MESH)
 
     at = pl.ds(pl.multiple_of(core * half, half), half)
     spots = ((wg, wgu.at[at, pl.ds(0, ffn)]), (wu, wgu.at[at, pl.ds(ffn, ffn)]), (wd, wdn.at[:, at]))
@@ -88,6 +89,17 @@
         w_copies.append(pltpu.make_async_copy(src, dst, w_loc.at[n]))
         w_copies.append(pltpu.make_async_remote_copy(src_ref=src, dst_ref=dst, send_sem=w_send.at[n], recv_sem=w_recv.at[n],
                                                      device_id={'fsdp': 1 - core}, device_id_type=MESH))
+
+    own = [pltpu.make_async_copy(tok_ref.at[:, pl.ds(cuts[a], cuts[a + 1] - cuts[a])], gathered[a].at[0], own_sem.at[a]) for a in range(3)]
+    for c in own:
+        c.start()
+    pl.semaphore_wait(barrier, 10)
+    for k in (2, 1, 3):
+        for a in range(3):
+            for c in ag_copies(a, k):
+                c.start()
+    for c in w_copies:
+        c.start()
 
     before = lax.broadcasted_iota(jnp.int32, (tok, tok), 0)
     after = lax.broadcasted_iota(jnp.int32, (tok, tok), 1)
@@ -229,10 +241,10 @@
             parts = jnp.dot(w, land[:, n:n + 512], preferred_element_type=F32)
             acc[:, n:n + 512] += parts[:tok] + parts[tok:2 * tok] + parts[2 * tok:]
 
-    acc[...] = tok_ref[...].astype(F32)
     for a in range(3):
-        gathered[a][0] = tok_ref[:, cuts[a]:cuts[a + 1]]
         plane_keys(a, 0)
+        own[a].wait()
+        acc[:, cuts[a]:cuts[a + 1]] = gathered[a][0].astype(F32)
     for k in (1, 3, 2):
         for a in range(3):
             for c in ag_copies(a, k):
@@ -240,8 +252,6 @@
             plane_keys(a, k)
     for g in range(LEAD):
         pick(jnp.int32(g))
-    for c in w_copies:
-        c.start()
     build_mix()
     for a in range(3):
         for k in (2, 1, 3):
@@ -286,7 +296,7 @@
         cap = (2 * tok * top_k + N_EXP - 1) // N_EXP
         cuts = (0, 640, 1280, dim)
         rows = PER * cap
-        idx_t = jnp.pad(expert_idx.T, ((0, 8 - top_k), (0, 0)))
+        idx_t = expert_idx.T
         gate_t = gates.T
         vmem = pl.BlockSpec(memory_space=pltpu.VMEM)
         hbm = pl.BlockSpec(memory_space=pl.ANY)
@@ -295,17 +305,17 @@
             functools.partial(layer_kernel, cap, cuts),
             out_shape=(jax.ShapeDtypeStruct((tok, dim), BF16), jax.ShapeDtypeStruct((2, GROUPS, rows, dim), BF16),
                        jax.ShapeDtypeStruct((3, GROUPS, rows, dim), BF16)),
-            in_specs=[vmem, vmem, vmem, hbm, hbm, hbm],
+            in_specs=[vmem, vmem, hbm, hbm, hbm, hbm],
             out_specs=(vmem, hbm, hbm),
             scratch_shapes=[pltpu.VMEM((dim, 2 * width), BF16), pltpu.VMEM((width, dim), BF16)]
             + [pltpu.VMEM((SIDE, tok, cuts[a + 1] - cuts[a]), BF16) for a in range(3)]
-            + [pltpu.VMEM((3, 3, 8, tok), jnp.int32), pltpu.VMEM((3, SIDE, 16, tok), F32), pltpu.VMEM((3 * tok, N_EXP * cap), BF16),
+            + [pltpu.VMEM((3, 3, top_k, tok), jnp.int32), pltpu.VMEM((3, SIDE, 16, tok), F32), pltpu.VMEM((3 * tok, N_EXP * cap), BF16),
                pltpu.VMEM((tok, dim), F32), pltpu.VMEM((RING, rows, dim), BF16), pltpu.VMEM((rows, dim), BF16),
                pltpu.VMEM((RING, rows, dim), BF16), pltpu.VMEM((rows, dim), BF16),
-               sem((3, 3)), sem((3, 3)), sem((3, 3)), sem((3, 3)), sem((3,)), sem((3,)), sem((3,)),
+               sem((3, 3)), sem((3, 3)), sem((3, 3)), sem((3, 3)), sem((3,)), sem((3,)), sem((3,)), sem((3,)),
                sem((RING,)), sem((GROUPS,)), sem((2, GROUPS)), sem,
                sem((RING,)), sem((GROUPS,)), sem((3, GROUPS)), sem((2,)), sem, sem],
-            compiler_params=pltpu.CompilerParams(has_side_effects=True, vmem_limit_bytes=63 * 1024 * 1024),
+            compiler_params=pltpu.CompilerParams(collective_id=0, has_side_effects=True, vmem_limit_bytes=63 * 1024 * 1024),
             name="moe_layer",
         )(idx_t, gate_t, tokens, w_gate[0], w_up[0], w_down[0])
         return out

time: 276 us -> 268 us (0.971)
  Pallas kernels: 271 us -> 264 us
    pallas_call x1, Pallas kernels: 271 us -> 264 us  [device_step(): pl.pallas_call(functools.partial(layer_kernel, cap, cuts), out_shape=(jax...]
where the time goes in v5:
time: 268 us; the launch traced here: 267 us
  Pallas kernels  264 us (99%)
    pallas_call x1, Pallas kernels, device_step(): pl.pallas_call(functools.partial(layer_kernel, cap, cuts), out_shape=(jax...  264 us

profile of v5, /device:TPU:0, one launch (start us, length us, event | category | flops | bytes accessed | tf_op | source)
XLA Modules:
  0.0 266.7 jit_solution(6935392486113211734)
XLA Ops:
  0.0 264.4 %moe_layer.1 = (bf16[256,2048]{1,0:T(8,128)(2,1)}, bf16[2,8,384,2048]{3,2,1,0:T(8,128)(2,1)}, bf16[3,8,384,2048]{3,2,1,0:T(8,128)(2,1)}) custom-call(s32[6,256]{1,0:T(8,128)} %bitcast.8, f32[6,256]{1,0:T(8,128)} %bitcast.9, bf16[256,2048]{1,0:T(8,128)(2,1)} %tok_ref.1, bf16[1024,1408]{1,0:T(8,128)(2,1)} %bitcast.5, bf16[1024,1408]{1,0:T(8,128)(2,1)} %bitcast.6, ...), custom_call_target="tpu_custom_call" | custom-call | tf_op jit(solution)/shard_map/moe_layer/pallas_call | solution.py:304
  264.4 2.3 copy.8

commit v6 on v5

--- a/solution.py
+++ b/solution.py
@@ -34,8 +34,11 @@
 
 def offset(g, i):
     dz, b = i // 2, i % 2
-    lean = 2 * b + lax.rem(g, 2)
-    return dz, lax.rem(dz + lean, SIDE), lax.rem(lean + lax.div(g, 2) + SIDE - dz, SIDE)
+    fixed = isinstance(g, int)
+    low, high = (g % 2, g // 2) if fixed else (lax.rem(g, 2), lax.div(g, 2))
+    lean = 2 * b + low
+    dy, dx = dz + lean, lean + high + SIDE - dz
+    return (dz, dy % SIDE, dx % SIDE) if fixed else (dz, lax.rem(dy, SIDE), lax.rem(dx, SIDE))
 
 
 def moved(d):
@@ -94,7 +97,7 @@
     for c in own:
         c.start()
     pl.semaphore_wait(barrier, 10)
-    for k in (2, 1, 3):
+    for k in (1, 3, 2):
         for a in range(3):
             for c in ag_copies(a, k):
                 c.start()
@@ -136,19 +139,26 @@
         def _():
             wait_rows(stage.at[ring], far, d_send.at[ring])
 
-        for i, p, d in each(g, OUT_ROUTES):
+        pick_blocks(g, ring, list(each(g, OUT_ROUTES)))
+
+    def pick_blocks(g, ring, blocks):
+        for i, p, d in blocks:
             lo, hi = cuts[p], cuts[p + 1]
             k = back_of(d[0])
             key = keys[p, k, pl.ds(back_of(d[1]) * 4 + back_of(d[2]), 1), :]
             sel = jnp.where(key == slot, 1.0, 0.0).astype(BF16)
             got = jnp.dot(sel, gathered[p][k], preferred_element_type=F32)
             stage[ring, i * cap:(i + 1) * cap, lo:hi] = got.astype(BF16)
-        for i, p, d in each(g, OUT_ROUTES):
+        for i, p, d in blocks:
             src, dst = stage.at[ring, *block(i, p)], inbox.at[0, g, *block(i, p)]
             if_moves(d[1], lambda: pltpu.make_async_remote_copy(
                 src_ref=src, dst_ref=dst, send_sem=d_send.at[ring], recv_sem=d_recv.at[0, g],
                 device_id={'ep': shifted(OUT_ROUTES[p][1], back_of(d[1]))}, device_id_type=MESH).start(),
                 lambda: pltpu.make_async_copy(src, dst, d_keep.at[g]).start())
+
+    def early_picks(k):
+        for g in range(LEAD):
+            pick_blocks(g, g, [(i, p, d) for i, p, d in each(g, OUT_ROUTES) if back_of(d[0]) == k])
 
     def forward(g):
         wait_rows(inbox.at[0, g], far, d_recv.at[0, g])
@@ -245,13 +255,13 @@
         plane_keys(a, 0)
         own[a].wait()
         acc[:, cuts[a]:cuts[a + 1]] = gathered[a][0].astype(F32)
+    early_picks(0)
     for k in (1, 3, 2):
         for a in range(3):
             for c in ag_copies(a, k):
                 c.wait_recv()
             plane_keys(a, k)
-    for g in range(LEAD):
-        pick(jnp.int32(g))
+        early_picks(k)
     build_mix()
     for a in range(3):
         for k in (2, 1, 3):

time: 268 us -> 264 us (0.985)
  Pallas kernels: 264 us -> 259 us
    pallas_call x1, Pallas kernels: 264 us -> 259 us  [device_step(): pl.pallas_call(functools.partial(layer_kernel, cap, cuts), out_shape=(jax...]
where the time goes in v6:
time: 264 us; the launch traced here: 261 us
  Pallas kernels  259 us (98%)
    pallas_call x1, Pallas kernels, device_step(): pl.pallas_call(functools.partial(layer_kernel, cap, cuts), out_shape=(jax...  259 us

profile of v6, /device:TPU:0, one launch (start us, length us, event | category | flops | bytes accessed | tf_op | source)
XLA Modules:
  0.0 261.1 jit_solution(9630641247342702225)
XLA Ops:
  0.0 258.8 %moe_layer.1 = (bf16[256,2048]{1,0:T(8,128)(2,1)}, bf16[2,8,384,2048]{3,2,1,0:T(8,128)(2,1)}, bf16[3,8,384,2048]{3,2,1,0:T(8,128)(2,1)}) custom-call(s32[6,256]{1,0:T(8,128)} %bitcast.8, f32[6,256]{1,0:T(8,128)} %bitcast.9, bf16[256,2048]{1,0:T(8,128)(2,1)} %tok_ref.1, bf16[1024,1408]{1,0:T(8,128)(2,1)} %bitcast.5, bf16[1024,1408]{1,0:T(8,128)(2,1)} %bitcast.6, ...), custom_call_target="tpu_custom_call" | custom-call | tf_op jit(solution)/shard_map/moe_layer/pallas_call | solution.py:314
  258.8 2.3 copy.8

commit v7 on v6

--- a/solution.py
+++ b/solution.py
@@ -54,9 +54,9 @@
         pl.when(d == 0)(near)
 
 
-def layer_kernel(cap, cuts, idx_ref, gate_ref, tok_ref, wg, wu, wd, out_ref, inbox, back,
-                 wgu, wdn, toks_z, toks_y, toks_x, idx_all, keys, mixw, acc, stage, xbuf, outs, land,
-                 ag_send, ag_recv, ix_send, ix_recv, own_sem, w_loc, w_send, w_recv,
+def layer_kernel(cap, cuts, idx_hbm, gate_hbm, tok_ref, wg, wu, wd, out_ref, inbox, back,
+                 wgu, wdn, toks_z, toks_y, toks_x, idx_all, idx_ref, gate_ref, keys, mixw, acc, stage, xbuf, outs, land,
+                 ag_send, ag_recv, ix_send, ix_recv, on_send, on_recv, own_sem, w_loc, w_send, w_recv,
                  d_send, d_keep, d_recv, d_relay, c_send, c_keep, c_recv, c_relay, x_sem, m_sem):
     tok, dim = acc.shape
     half, ffn = wg.shape
@@ -73,11 +73,18 @@
     def ag_copies(a, k):
         dev = {'ep': shifted(a, k)}
         lo, hi = cuts[a], cuts[a + 1]
-        yield pltpu.make_async_remote_copy(src_ref=idx_ref, dst_ref=idx_all.at[a, k - 1], send_sem=ix_send.at[a, k - 1],
+        yield pltpu.make_async_remote_copy(src_ref=idx_hbm, dst_ref=idx_all.at[a, k - 1], send_sem=ix_send.at[a, k - 1],
                                            recv_sem=ix_recv.at[a, k - 1], device_id=dev, device_id_type=MESH)
-        yield pltpu.make_async_remote_copy(src_ref=tok_ref.at[:, pl.ds(lo, hi - lo)], dst_ref=gathered[a].at[k],
-                                           send_sem=ag_send.at[a, k - 1], recv_sem=ag_recv.at[a, k - 1],
-                                           device_id=dev, device_id_type=MESH)
+        if k != 2:
+            yield pltpu.make_async_remote_copy(src_ref=tok_ref.at[:, pl.ds(lo, hi - lo)], dst_ref=gathered[a].at[k],
+                                               send_sem=ag_send.at[a, k - 1], recv_sem=ag_recv.at[a, k - 1],
+                                               device_id=dev, device_id_type=MESH)
+
+    def pass_on(a, k):
+        part = pl.ds(0 if k == 1 else tok // 2, tok // 2)
+        return pltpu.make_async_remote_copy(src_ref=gathered[a].at[k, part], dst_ref=gathered[a].at[2, part],
+                                            send_sem=on_send.at[a, k // 2], recv_sem=on_recv.at[a, k // 2],
+                                            device_id={'ep': shifted(a, k)}, device_id_type=MESH)
 
     barrier = pltpu.get_barrier_semaphore()
     for a in range(3):
@@ -94,7 +101,8 @@
                                                      device_id={'fsdp': 1 - core}, device_id_type=MESH))
 
     own = [pltpu.make_async_copy(tok_ref.at[:, pl.ds(cuts[a], cuts[a + 1] - cuts[a])], gathered[a].at[0], own_sem.at[a]) for a in range(3)]
-    for c in own:
+    own += [pltpu.make_async_copy(idx_hbm, idx_ref, own_sem.at[3]), pltpu.make_async_copy(gate_hbm, gate_ref, own_sem.at[4])]
+    for c in own[::-1]:
         c.start()
     pl.semaphore_wait(barrier, 10)
     for k in (1, 3, 2):
@@ -251,15 +259,25 @@
             parts = jnp.dot(w, land[:, n:n + 512], preferred_element_type=F32)
             acc[:, n:n + 512] += parts[:tok] + parts[tok:2 * tok] + parts[2 * tok:]
 
+    own[3].wait()
+    own[4].wait()
     for a in range(3):
         plane_keys(a, 0)
         own[a].wait()
         acc[:, cuts[a]:cuts[a + 1]] = gathered[a][0].astype(F32)
     early_picks(0)
-    for k in (1, 3, 2):
+    for k in (1, 3):
         for a in range(3):
             for c in ag_copies(a, k):
                 c.wait_recv()
+            pass_on(a, k).start()
+    for k in (1, 3, 2):
+        for a in range(3):
+            if k == 2:
+                for c in ag_copies(a, k):
+                    c.wait_recv()
+                pass_on(a, 1).wait_recv()
+                pass_on(a, 3).wait_recv()
             plane_keys(a, k)
         early_picks(k)
     build_mix()
@@ -267,6 +285,8 @@
         for k in (2, 1, 3):
             for c in ag_copies(a, k):
                 c.wait_send()
+        pass_on(a, 1).wait_send()
+        pass_on(a, 3).wait_send()
 
     def in_turn(r, lag, step):
         g = r - lag
@@ -315,14 +335,14 @@
             functools.partial(layer_kernel, cap, cuts),
             out_shape=(jax.ShapeDtypeStruct((tok, dim), BF16), jax.ShapeDtypeStruct((2, GROUPS, rows, dim), BF16),
                        jax.ShapeDtypeStruct((3, GROUPS, rows, dim), BF16)),
-            in_specs=[vmem, vmem, hbm, hbm, hbm, hbm],
+            in_specs=[hbm] * 6,
             out_specs=(vmem, hbm, hbm),
             scratch_shapes=[pltpu.VMEM((dim, 2 * width), BF16), pltpu.VMEM((width, dim), BF16)]
             + [pltpu.VMEM((SIDE, tok, cuts[a + 1] - cuts[a]), BF16) for a in range(3)]
-            + [pltpu.VMEM((3, 3, top_k, tok), jnp.int32), pltpu.VMEM((3, SIDE, 16, tok), F32), pltpu.VMEM((3 * tok, N_EXP * cap), BF16),
+            + [pltpu.VMEM((3, 3, top_k, tok), jnp.int32), pltpu.VMEM((top_k, tok), jnp.int32), pltpu.VMEM((top_k, tok), F32), pltpu.VMEM((3, SIDE, 16, tok), F32), pltpu.VMEM((3 * tok, N_EXP * cap), BF16),
                pltpu.VMEM((tok, dim), F32), pltpu.VMEM((RING, rows, dim), BF16), pltpu.VMEM((rows, dim), BF16),
                pltpu.VMEM((RING, rows, dim), BF16), pltpu.VMEM((rows, dim), BF16),
-               sem((3, 3)), sem((3, 3)), sem((3, 3)), sem((3, 3)), sem((3,)), sem((3,)), sem((3,)), sem((3,)),
+               sem((3, 3)), sem((3, 3)), sem((3, 3)), sem((3, 3)), sem((3, 2)), sem((3, 2)), sem((5,)), sem((3,)), sem((3,)), sem((3,)),
                sem((RING,)), sem((GROUPS,)), sem((2, GROUPS)), sem,
                sem((RING,)), sem((GROUPS,)), sem((3, GROUPS)), sem((2,)), sem, sem],
             compiler_params=pltpu.CompilerParams(collective_id=0, has_side_effects=True, vmem_limit_bytes=63 * 1024 * 1024),

time: 264 us -> 259 us (0.981)
  Pallas kernels: 259 us -> 255 us
    pallas_call x1, Pallas kernels: 259 us -> 255 us  [device_step(): pl.pallas_call(functools.partial(layer_kernel, cap, cuts), out_shape=(jax...]
where the time goes in v7:
time: 259 us; the launch traced here: 257 us
  Pallas kernels  255 us (98%)
    pallas_call x1, Pallas kernels, device_step(): pl.pallas_call(functools.partial(layer_kernel, cap, cuts), out_shape=(jax...  255 us

profile of v7, /device:TPU:0, one launch (start us, length us, event | category | flops | bytes accessed | tf_op | source)
XLA Modules:
  0.0 256.9 jit_solution(2344047654821879999)
XLA Ops:
  0.0 254.6 %moe_layer.1 = (bf16[256,2048]{1,0:T(8,128)(2,1)}, bf16[2,8,384,2048]{3,2,1,0:T(8,128)(2,1)}, bf16[3,8,384,2048]{3,2,1,0:T(8,128)(2,1)}) custom-call(s32[6,256]{1,0:T(8,128)} %bitcast.8, f32[6,256]{1,0:T(8,128)} %bitcast.9, bf16[256,2048]{1,0:T(8,128)(2,1)} %tok_ref.1, bf16[1024,1408]{1,0:T(8,128)(2,1)} %bitcast.5, bf16[1024,1408]{1,0:T(8,128)(2,1)} %bitcast.6, ...), custom_call_target="tpu_custom_call" | custom-call | tf_op jit(solution)/shard_map/moe_layer/pallas_call | solution.py:334
  254.6 2.3 copy.8

commit v8 on v7

--- a/solution.py
+++ b/solution.py
@@ -17,7 +17,7 @@
 ROUTES = ((2, 1, 0), (1, 0, 2), (0, 2, 1))
 OUT_ROUTES = ((0, 1, 2), (1, 2, 0), (2, 0, 1))
 LEAD = 3
-RING = 4
+RING = 3
 
 
 def hits(idx_t, eid):
@@ -55,10 +55,10 @@
 
 
 def layer_kernel(cap, cuts, idx_hbm, gate_hbm, tok_ref, wg, wu, wd, out_ref, inbox, back,
-                 wgu, wdn, toks_z, toks_y, toks_x, idx_all, idx_ref, gate_ref, keys, mixw, acc, stage, xbuf, outs, land,
-                 ag_send, ag_recv, ix_send, ix_recv, on_send, on_recv, own_sem, w_loc, w_send, w_recv,
-                 d_send, d_keep, d_recv, d_relay, c_send, c_keep, c_recv, c_relay, x_sem, m_sem):
-    tok, dim = acc.shape
+                 wgu, wdn, toks_z, toks_y, toks_x, idx_all, gate_all, idx_ref, gate_ref, keys, gates, acc, partial, stage, xbuf, outs, land,
+                 ag_send, ag_recv, ix_send, ix_recv, gt_send, gt_recv, on_send, on_recv, own_sem, w_loc, w_send, w_recv,
+                 d_send, d_keep, d_recv, d_relay, c_send, c_keep, c_recv, c_relay, p_send, p_recv, x_sem, m_sem):
+    tok, dim = acc.shape[1:]
     half, ffn = wg.shape
     rows = PER * cap
     far = rows // SIDE * (SIDE - 1)
@@ -75,6 +75,8 @@
         lo, hi = cuts[a], cuts[a + 1]
         yield pltpu.make_async_remote_copy(src_ref=idx_hbm, dst_ref=idx_all.at[a, k - 1], send_sem=ix_send.at[a, k - 1],
                                            recv_sem=ix_recv.at[a, k - 1], device_id=dev, device_id_type=MESH)
+        yield pltpu.make_async_remote_copy(src_ref=gate_hbm, dst_ref=gate_all.at[a, k - 1], send_sem=gt_send.at[a, k - 1],
+                                           recv_sem=gt_recv.at[a, k - 1], device_id=dev, device_id_type=MESH)
         if k != 2:
             yield pltpu.make_async_remote_copy(src_ref=tok_ref.at[:, pl.ds(lo, hi - lo)], dst_ref=gathered[a].at[k],
                                                send_sem=ag_send.at[a, k - 1], recv_sem=ag_recv.at[a, k - 1],
@@ -136,6 +138,11 @@
         eid = pos[a] * STRIDE[a] + ((pos[b] + (q >> 2)) & 3) * STRIDE[b] + ((pos[c] + (q & 3)) & 3) * STRIDE[c]
         ids = idx_ref[...] if k == 0 else idx_all[a, k - 1]
         keys[a, k] = slot_keys(hits(ids, eid), earlier)
+        gate = gate_ref[...] if k == 0 else gate_all[a, k - 1]
+        mine = jnp.zeros((16, tok), F32)
+        for j in range(6):
+            mine = jnp.where(ids[j:j + 1, :] == eid, gate[j:j + 1, :], mine)
+        gates[a, k] = mine
 
     def back_of(d):
         return (SIDE - d) % SIDE if isinstance(d, int) else lax.rem(SIDE - d, SIDE)
@@ -181,39 +188,6 @@
         for i, p, d in each(g, OUT_ROUTES):
             pltpu.make_async_copy(inbox.at[moved(d[2]), g, *block(i, p)], xbuf.at[block(i, p)], x_sem).start()
 
-    def build_mix():
-        idx_t, gate_t = idx_ref[...], gate_ref[...]
-        eid = lax.broadcasted_iota(jnp.int32, (N_EXP, tok), 0)
-        key = slot_keys(hits(idx_t, eid), earlier).astype(BF16)
-        gate = jnp.zeros((N_EXP, tok), F32)
-        for j in range(6):
-            gate = jnp.where(idx_t[j:j + 1, :] == eid, gate_t[j:j + 1, :], gate)
-        pieces = []
-        left = gate
-        for part in range(3):
-            pieces.append(left.astype(BF16))
-            left = left - pieces[-1].astype(F32)
-        turn = functools.partial(lax.dot_general, dimension_numbers=(((0,), (0,)), ((), ())), preferred_element_type=F32)
-        col = lax.broadcasted_iota(jnp.int32, (N_EXP, rows), 1)
-        row = lax.broadcasted_iota(jnp.int32, (N_EXP, rows), 0)
-        nth = jnp.zeros((N_EXP, rows), jnp.int32)
-        for n in range(1, PER):
-            nth = nth + jnp.where(col >= n * cap, 1, 0)
-        want = (col - nth * cap)[0:1].astype(F32)
-        dz = nth >> 1
-
-        @pl.loop(0, GROUPS)
-        def _(g):
-            lean = (nth & 1) * 2 + lax.rem(g, 2)
-            dy = (dz + lean) & 3
-            dx = (lean + lax.div(g, 2) - dz) & 3
-            exp = ((pos[0] - dz) & 3) * 16 + ((pos[1] - dy) & 3) * 4 + ((pos[2] - dx) & 3)
-            spread = jnp.where(exp == row, 1.0, 0.0).astype(BF16)
-            mine = turn(key, spread) == want
-            span = pl.ds(pl.multiple_of(g * rows, 128), rows)
-            for part in range(3):
-                mixw[part * tok:(part + 1) * tok, span] = jnp.where(mine, turn(pieces[part], spread), 0.0).astype(BF16)
-
     def experts(g):
         ring = lax.rem(g, RING)
         pltpu.make_async_copy(xbuf, xbuf, x_sem).wait()
@@ -240,32 +214,75 @@
         wait_rows(back.at[0, g], far, c_recv.at[0, g])
         wait_rows(back.at[0, g], rows - far, c_keep.at[g])
         for i, p, d in each(g, ROUTES):
-            if_moves(d[1], lambda: hop(back.at[0, g, *block(i, p)], 1, g, i, p, d[1], c_relay.at[0]).start())
-
-    def third_hops(g):
-        wait_rows(back.at[1, g], far, c_recv.at[1, g])
-        for i, p, d in each(g, ROUTES):
-            if_moves(d[2], lambda: hop(back.at[moved(d[1]), g, *block(i, p)], 2, g, i, p, d[2], c_relay.at[1]).start())
-
-    def mix(g):
-        wait_rows(back.at[2, g], far, c_recv.at[2, g])
-        for i, p, d in each(g, ROUTES):
-            last = moved(d[2])
-            leg = 2 * last + (1 - last) * moved(d[1])
-            pltpu.make_async_copy(back.at[leg, g, *block(i, p)], land.at[block(i, p)], m_sem).start()
+            if_moves(d[1], lambda: hop(back.at[0, g, *block(i, p)], 1, g, i, p, d[1], c_relay).start())
+
+    def partial_copy(p, d):
+        span = pl.ds(cuts[p], cuts[p + 1] - cuts[p])
+        return pltpu.make_async_remote_copy(
+            src_ref=acc.at[d, :, span], dst_ref=partial.at[d - 1, :, span], send_sem=p_send.at[p, d - 1],
+            recv_sem=p_recv.at[p, d - 1], device_id={'ep': shifted(ROUTES[p][2], d)}, device_id_type=MESH)
+
+    def quarter(x):
+        return x % SIDE if isinstance(x, int) else lax.rem(x + 2 * SIDE, SIDE)
+
+    def members(m, p, d):
+        for n in range(4):
+            odd, b = n // 2, n % 2
+            lean = 2 * b + odd
+            axis = ROUTES[p][2]
+            dz = d if axis == 0 else quarter(d - lean) if axis == 1 else quarter(lean + m - d)
+            dy = d if axis == 1 else quarter(dz + lean)
+            dx = d if axis == 2 else quarter(lean + m - dz)
+            yield n, 2 * m + odd, 2 * dz + b, (dz, dy, dx)
+
+    def mix(m):
+        for odd in range(2):
+            wait_rows(back.at[1, 2 * m + odd], far, c_recv.at[1, 2 * m + odd])
+        for d in range(SIDE):
+            for p in range(3):
+                span = pl.ds(cuts[p], cuts[p + 1] - cuts[p])
+                for n, g, i, ds in members(m, p, d):
+                    start = i * cap if isinstance(i, int) else pl.multiple_of(i * cap, cap)
+                    pltpu.make_async_copy(back.at[moved(ds[ROUTES[p][1]]), g, pl.ds(start, cap), span],
+                                          land.at[pl.ds((4 * d + n) * cap, cap), span], m_sem).start()
         pltpu.make_async_copy(land, land, m_sem).wait()
-        w = mixw[:, pl.ds(pl.multiple_of(g * rows, 128), rows)]
-        for n in range(0, dim, 512):
-            parts = jnp.dot(w, land[:, n:n + 512], preferred_element_type=F32)
-            acc[:, n:n + 512] += parts[:tok] + parts[tok:2 * tok] + parts[2 * tok:]
+        for d in (2, 1, 3, 0):
+            for p in range(3):
+                lo, hi = cuts[p], cuts[p + 1]
+                a = ROUTES[p][2]
+                _, b, c = OUT_ROUTES[a]
+                tall = []
+                for n, g, i, ds in members(m, p, d):
+                    row = pl.ds(back_of(ds[b]) * 4 + back_of(ds[c]), 1)
+                    here = keys[a, (SIDE - d) % SIDE, row, :] == slot
+                    left = gates[a, (SIDE - d) % SIDE, row, :]
+                    wide = []
+                    for _ in range(3):
+                        piece = left.astype(BF16).astype(F32)
+                        left = left - piece
+                        wide.append(jnp.where(here, piece, 0.0))
+                    tall.append(jnp.concatenate(wide, axis=1))
+                weight = jnp.concatenate(tall, axis=0).astype(BF16)
+                parts = lax.dot_general(weight, land[4 * d * cap:4 * (d + 1) * cap, lo:hi], (((0,), (0,)), ((), ())),
+                                        preferred_element_type=F32)
+                acc[d, :, lo:hi] += parts[:tok] + parts[tok:2 * tok] + parts[2 * tok:]
+            if d:
+                @pl.when(m == GROUPS // 2 - 1)
+                def _():
+                    for p in range(3):
+                        partial_copy(p, d).start()
+
+    def mix_odd(g):
+        pl.when(lax.rem(g, 2) == 1)(lambda: mix(lax.div(g, 2)))
 
     own[3].wait()
     own[4].wait()
     for a in range(3):
         plane_keys(a, 0)
         own[a].wait()
-        acc[:, cuts[a]:cuts[a + 1]] = gathered[a][0].astype(F32)
+        acc[0, :, cuts[a]:cuts[a + 1]] = gathered[a][0].astype(F32)
     early_picks(0)
+    acc[1:] = jnp.zeros((SIDE - 1, tok, dim), F32)
     for k in (1, 3):
         for a in range(3):
             for c in ag_copies(a, k):
@@ -280,7 +297,6 @@
                 pass_on(a, 3).wait_recv()
             plane_keys(a, k)
         early_picks(k)
-    build_mix()
     for a in range(3):
         for k in (2, 1, 3):
             for c in ag_copies(a, k):
@@ -292,7 +308,7 @@
         g = r - lag
         pl.when((g >= 0) & (g < GROUPS))(lambda: step(g))
 
-    @pl.loop(0, GROUPS + 4)
+    @pl.loop(0, GROUPS + 3)
     def _(r):
         @pl.when(r == 1)
         def _():
@@ -304,14 +320,17 @@
         pl.when(r + LEAD < GROUPS)(lambda: pick(r + LEAD))
         in_turn(r, 1, experts)
         in_turn(r, 2, second_hops)
-        in_turn(r, 3, third_hops)
-        in_turn(r, 4, mix)
-
-    out_ref[...] = acc[...].astype(BF16)
+        in_turn(r, 3, mix_odd)
+
+    for p in range(3):
+        lo, hi = cuts[p], cuts[p + 1]
+        for d in (1, 3, 2):
+            partial_copy(p, d).wait()
+        out_ref[:, lo:hi] = (acc[0, :, lo:hi] + partial[0, :, lo:hi] + partial[1, :, lo:hi] + partial[2, :, lo:hi]).astype(BF16)
     for ring in range(RING):
         wait_rows(stage.at[ring], far, d_send.at[ring])
         wait_rows(outs.at[ring], far, c_send.at[ring])
-    for sem in (d_relay, c_relay.at[0], c_relay.at[1]):
+    for sem in (d_relay, c_relay):
         part = back.at[0, :, pl.ds(0, far)]
         pltpu.make_async_copy(part, part, sem).wait()
 
@@ -334,17 +353,18 @@
         out, _, _ = pl.pallas_call(
             functools.partial(layer_kernel, cap, cuts),
             out_shape=(jax.ShapeDtypeStruct((tok, dim), BF16), jax.ShapeDtypeStruct((2, GROUPS, rows, dim), BF16),
-                       jax.ShapeDtypeStruct((3, GROUPS, rows, dim), BF16)),
+                       jax.ShapeDtypeStruct((2, GROUPS, rows, dim), BF16)),
             in_specs=[hbm] * 6,
             out_specs=(vmem, hbm, hbm),
             scratch_shapes=[pltpu.VMEM((dim, 2 * width), BF16), pltpu.VMEM((width, dim), BF16)]
             + [pltpu.VMEM((SIDE, tok, cuts[a + 1] - cuts[a]), BF16) for a in range(3)]
-            + [pltpu.VMEM((3, 3, top_k, tok), jnp.int32), pltpu.VMEM((top_k, tok), jnp.int32), pltpu.VMEM((top_k, tok), F32), pltpu.VMEM((3, SIDE, 16, tok), F32), pltpu.VMEM((3 * tok, N_EXP * cap), BF16),
-               pltpu.VMEM((tok, dim), F32), pltpu.VMEM((RING, rows, dim), BF16), pltpu.VMEM((rows, dim), BF16),
-               pltpu.VMEM((RING, rows, dim), BF16), pltpu.VMEM((rows, dim), BF16),
-               sem((3, 3)), sem((3, 3)), sem((3, 3)), sem((3, 3)), sem((3, 2)), sem((3, 2)), sem((5,)), sem((3,)), sem((3,)), sem((3,)),
+            + [pltpu.VMEM((3, 3, top_k, tok), jnp.int32), pltpu.VMEM((3, 3, top_k, tok), F32), pltpu.VMEM((top_k, tok), jnp.int32), pltpu.VMEM((top_k, tok), F32), pltpu.VMEM((3, SIDE, 16, tok), F32), pltpu.VMEM((3, SIDE, 16, tok), F32),
+               pltpu.VMEM((SIDE, tok, dim), F32), pltpu.VMEM((SIDE - 1, tok, dim), F32), pltpu.VMEM((RING, rows, dim), BF16),
+               pltpu.VMEM((rows, dim), BF16), pltpu.VMEM((RING, rows, dim), BF16), pltpu.VMEM((2 * rows, dim), BF16),
+               sem((3, 3)), sem((3, 3)), sem((3, 3)), sem((3, 3)), sem((3, 3)), sem((3, 3)), sem((3, 2)), sem((3, 2)), sem((5,)),
+               sem((3,)), sem((3,)), sem((3,)),
                sem((RING,)), sem((GROUPS,)), sem((2, GROUPS)), sem,
-               sem((RING,)), sem((GROUPS,)), sem((3, GROUPS)), sem((2,)), sem, sem],
+               sem((RING,)), sem((GROUPS,)), sem((2, GROUPS)), sem, sem((3, 3)), sem((3, 3)), sem, sem],
             compiler_params=pltpu.CompilerParams(collective_id=0, has_side_effects=True, vmem_limit_bytes=63 * 1024 * 1024),
             name="moe_layer",
         )(idx_t, gate_t, tokens, w_gate[0], w_up[0], w_down[0])

time: 259 us -> 252 us (0.973)
  Pallas kernels: 255 us -> 248 us
    pallas_call x1, Pallas kernels: 255 us -> 248 us  [device_step(): pl.pallas_call(functools.partial(layer_kernel, cap, cuts), out_shape=(jax...]
where the time goes in v8:
time: 252 us; the launch traced here: 250 us
  Pallas kernels  248 us (98%)
    pallas_call x1, Pallas kernels, device_step(): pl.pallas_call(functools.partial(layer_kernel, cap, cuts), out_shape=(jax...  248 us

profile of v8, /device:TPU:0, one launch (start us, length us, event | category | flops | bytes accessed | tf_op | source)
XLA Modules:
  0.0 250.4 jit_solution(16446507375185274667)
XLA Ops:
  0.0 248.1 %moe_layer.1 = (bf16[256,2048]{1,0:T(8,128)(2,1)}, bf16[2,8,384,2048]{3,2,1,0:T(8,128)(2,1)}, bf16[2,8,384,2048]{3,2,1,0:T(8,128)(2,1)}) custom-call(s32[6,256]{1,0:T(8,128)} %bitcast.8, f32[6,256]{1,0:T(8,128)} %bitcast.9, bf16[256,2048]{1,0:T(8,128)(2,1)} %tok_ref.1, bf16[1024,1408]{1,0:T(8,128)(2,1)} %bitcast.5, bf16[1024,1408]{1,0:T(8,128)(2,1)} %bitcast.6, ...), custom_call_target="tpu_custom_call" | custom-call | tf_op jit(solution)/shard_map/moe_layer/pallas_call | solution.py:353
  248.1 2.3 copy.8

commit v9 on v8

--- a/solution.py
+++ b/solution.py
@@ -57,7 +57,7 @@
 def layer_kernel(cap, cuts, idx_hbm, gate_hbm, tok_ref, wg, wu, wd, out_ref, inbox, back,
                  wgu, wdn, toks_z, toks_y, toks_x, idx_all, gate_all, idx_ref, gate_ref, keys, gates, acc, partial, stage, xbuf, outs, land,
                  ag_send, ag_recv, ix_send, ix_recv, gt_send, gt_recv, on_send, on_recv, own_sem, w_loc, w_send, w_recv,
-                 d_send, d_keep, d_recv, d_relay, c_send, c_keep, c_recv, c_relay, p_send, p_recv, x_sem, m_sem):
+                 d_send, d_keep, d_recv, d_relay, c_send, c_keep, c_recv, c_relay, j_send, j_recv, p_send, p_recv, x_sem, m_sem):
     tok, dim = acc.shape[1:]
     half, ffn = wg.shape
     rows = PER * cap
@@ -216,11 +216,23 @@
         for i, p, d in each(g, ROUTES):
             if_moves(d[1], lambda: hop(back.at[0, g, *block(i, p)], 1, g, i, p, d[1], c_relay).start())
 
-    def partial_copy(p, d):
-        span = pl.ds(cuts[p], cuts[p + 1] - cuts[p])
+    def partial_copy(p, d, part):
+        where = (pl.ds(part * (tok // 2), tok // 2), pl.ds(cuts[p], cuts[p + 1] - cuts[p]))
+        if d == 2:
+            step, sems = (1, 3)[part], (j_send.at[p, part], j_recv.at[p, part])
+        else:
+            step, sems = d, (p_send.at[p, d // 2, part], p_recv.at[p, d // 2, part])
         return pltpu.make_async_remote_copy(
-            src_ref=acc.at[d, :, span], dst_ref=partial.at[d - 1, :, span], send_sem=p_send.at[p, d - 1],
-            recv_sem=p_recv.at[p, d - 1], device_id={'ep': shifted(ROUTES[p][2], d)}, device_id_type=MESH)
+            src_ref=acc.at[d, *where], dst_ref=partial.at[d - 1, *where], send_sem=sems[0], recv_sem=sems[1],
+            device_id={'ep': shifted(ROUTES[p][2], step)}, device_id_type=MESH)
+
+    def join(p):
+        lo, hi = cuts[p], cuts[p + 1]
+        for part, d in ((0, 1), (1, 3)):
+            span = slice(part * (tok // 2), (part + 1) * (tok // 2))
+            partial_copy(p, 2, part).wait_recv()
+            acc[d, span, lo:hi] += partial[1, span, lo:hi]
+            partial_copy(p, d, part).start()
 
     def quarter(x):
         return x % SIDE if isinstance(x, int) else lax.rem(x + 2 * SIDE, SIDE)
@@ -270,7 +282,8 @@
                 @pl.when(m == GROUPS // 2 - 1)
                 def _():
                     for p in range(3):
-                        partial_copy(p, d).start()
+                        for part in ((0, 1) if d == 2 else (1,) if d == 1 else (0,)):
+                            partial_copy(p, d, part).start()
 
     def mix_odd(g):
         pl.when(lax.rem(g, 2) == 1)(lambda: mix(lax.div(g, 2)))
@@ -323,10 +336,14 @@
         in_turn(r, 3, mix_odd)
 
     for p in range(3):
+        join(p)
+    for p in range(3):
         lo, hi = cuts[p], cuts[p + 1]
-        for d in (1, 3, 2):
-            partial_copy(p, d).wait()
-        out_ref[:, lo:hi] = (acc[0, :, lo:hi] + partial[0, :, lo:hi] + partial[1, :, lo:hi] + partial[2, :, lo:hi]).astype(BF16)
+        for part in range(2):
+            partial_copy(p, 2, part).wait_send()
+            for d in (1, 3):
+                partial_copy(p, d, part).wait()
+        out_ref[:, lo:hi] = (acc[0, :, lo:hi] + partial[0, :, lo:hi] + partial[2, :, lo:hi]).astype(BF16)
     for ring in range(RING):
         wait_rows(stage.at[ring], far, d_send.at[ring])
         wait_rows(outs.at[ring], far, c_send.at[ring])
@@ -364,7 +381,7 @@
                sem((3, 3)), sem((3, 3)), sem((3, 3)), sem((3, 3)), sem((3, 3)), sem((3, 3)), sem((3, 2)), sem((3, 2)), sem((5,)),
                sem((3,)), sem((3,)), sem((3,)),
                sem((RING,)), sem((GROUPS,)), sem((2, GROUPS)), sem,
-               sem((RING,)), sem((GROUPS,)), sem((2, GROUPS)), sem, sem((3, 3)), sem((3, 3)), sem, sem],
+               sem((RING,)), sem((GROUPS,)), sem((2, GROUPS)), sem, sem((3, 2)), sem((3, 2)), sem((3, 2, 2)), sem((3, 2, 2)), sem, sem],
             compiler_params=pltpu.CompilerParams(collective_id=0, has_side_effects=True, vmem_limit_bytes=63 * 1024 * 1024),
             name="moe_layer",
         )(idx_t, gate_t, tokens, w_gate[0], w_up[0], w_down[0])

time: 252 us -> 242 us (0.960)
  Pallas kernels: 248 us -> 240 us
    pallas_call x1, Pallas kernels: 248 us -> 240 us  [device_step(): pl.pallas_call(functools.partial(layer_kernel, cap, cuts), out_shape=(jax...]
where the time goes in v9:
time: 242 us
  Pallas kernels  240 us (99%)
    pallas_call x1, Pallas kernels, device_step(): pl.pallas_call(functools.partial(layer_kernel, cap, cuts), out_shape=(jax...  240 us

profile of v9, /device:TPU:0, one launch (start us, length us, event | category | flops | bytes accessed | tf_op | source)
XLA Modules:
  0.0 241.8 jit_solution(7502871361790101516)
XLA Ops:
  0.0 239.5 %moe_layer.1 = (bf16[256,2048]{1,0:T(8,128)(2,1)}, bf16[2,8,384,2048]{3,2,1,0:T(8,128)(2,1)}, bf16[2,8,384,2048]{3,2,1,0:T(8,128)(2,1)}) custom-call(s32[6,256]{1,0:T(8,128)} %bitcast.8, f32[6,256]{1,0:T(8,128)} %bitcast.9, bf16[256,2048]{1,0:T(8,128)(2,1)} %tok_ref.1, bf16[1024,1408]{1,0:T(8,128)(2,1)} %bitcast.5, bf16[1024,1408]{1,0:T(8,128)(2,1)} %bitcast.6, ...), custom_call_target="tpu_custom_call" | custom-call | tf_op jit(solution)/shard_map/moe_layer/pallas_call | solution.py:370
  239.5 2.3 copy.8

commit v10 on v9

--- a/solution.py
+++ b/solution.py
@@ -250,16 +250,16 @@
     def mix(m):
         for odd in range(2):
             wait_rows(back.at[1, 2 * m + odd], far, c_recv.at[1, 2 * m + odd])
-        for d in range(SIDE):
-            for p in range(3):
-                span = pl.ds(cuts[p], cuts[p + 1] - cuts[p])
-                for n, g, i, ds in members(m, p, d):
-                    start = i * cap if isinstance(i, int) else pl.multiple_of(i * cap, cap)
-                    pltpu.make_async_copy(back.at[moved(ds[ROUTES[p][1]]), g, pl.ds(start, cap), span],
-                                          land.at[pl.ds((4 * d + n) * cap, cap), span], m_sem).start()
+            for d in range(SIDE):
+                for p in range(3):
+                    span = pl.ds(cuts[p], cuts[p + 1] - cuts[p])
+                    for n, g, i, ds in list(members(m, p, d))[2 * odd:2 * odd + 2]:
+                        start = i * cap if isinstance(i, int) else pl.multiple_of(i * cap, cap)
+                        pltpu.make_async_copy(back.at[moved(ds[ROUTES[p][1]]), g, pl.ds(start, cap), span],
+                                              land.at[pl.ds((4 * d + n) * cap, cap), span], m_sem).start()
         pltpu.make_async_copy(land, land, m_sem).wait()
         for d in (2, 1, 3, 0):
-            for p in range(3):
+            for p in (2, 0, 1):
                 lo, hi = cuts[p], cuts[p + 1]
                 a = ROUTES[p][2]
                 _, b, c = OUT_ROUTES[a]
@@ -278,10 +278,9 @@
                 parts = lax.dot_general(weight, land[4 * d * cap:4 * (d + 1) * cap, lo:hi], (((0,), (0,)), ((), ())),
                                         preferred_element_type=F32)
                 acc[d, :, lo:hi] += parts[:tok] + parts[tok:2 * tok] + parts[2 * tok:]
-            if d:
-                @pl.when(m == GROUPS // 2 - 1)
-                def _():
-                    for p in range(3):
+                if d:
+                    @pl.when(m == GROUPS // 2 - 1)
+                    def _():
                         for part in ((0, 1) if d == 2 else (1,) if d == 1 else (0,)):
                             partial_copy(p, d, part).start()
 
@@ -335,9 +334,9 @@
         in_turn(r, 2, second_hops)
         in_turn(r, 3, mix_odd)
 
-    for p in range(3):
+    for p in (2, 0, 1):
         join(p)
-    for p in range(3):
+    for p in (0, 1, 2):
         lo, hi = cuts[p], cuts[p + 1]
         for part in range(2):
             partial_copy(p, 2, part).wait_send()

time: 242 us -> 241 us (level)
  no operation moved by 1% of the time
where the time goes in v10:
time: 241 us
  Pallas kernels  238 us (99%)
    pallas_call x1, Pallas kernels, device_step(): pl.pallas_call(functools.partial(layer_kernel, cap, cuts), out_shape=(jax...  238 us

profile of v10, /device:TPU:0, one launch (start us, length us, event | category | flops | bytes accessed | tf_op | source)
XLA Modules:
  0.0 240.7 jit_solution(17507070928602445190)
XLA Ops:
  0.0 238.4 %moe_layer.1 = (bf16[256,2048]{1,0:T(8,128)(2,1)}, bf16[2,8,384,2048]{3,2,1,0:T(8,128)(2,1)}, bf16[2,8,384,2048]{3,2,1,0:T(8,128)(2,1)}) custom-call(s32[6,256]{1,0:T(8,128)} %bitcast.8, f32[6,256]{1,0:T(8,128)} %bitcast.9, bf16[256,2048]{1,0:T(8,128)(2,1)} %tok_ref.1, bf16[1024,1408]{1,0:T(8,128)(2,1)} %bitcast.5, bf16[1024,1408]{1,0:T(8,128)(2,1)} %bitcast.6, ...), custom_call_target="tpu_custom_call" | custom-call | tf_op jit(solution)/shard_map/moe_layer/pallas_call | solution.py:369
  238.4 2.3 copy.8
